TPU v7x, 32 devices: a whole 2x2x4 slice. The times are simulated.
32 devices in a mesh: dp: 8 (over z, x), heads: 4 (over y, core).
Axes of the slice: x: 2, y: 2, z: 4, core: 2. Of those that a mesh axis runs over, the one named last changes fastest.
Arguments:
- queries: bfloat16 [64, 16, 128], P('dp', 'heads'), may hold values from -12 to 12
- key_cache: bfloat16 [512, 8, 256, 128], P('dp', 'heads'), may hold values from -6 to 6
- value_cache: bfloat16 [512, 8, 256, 128], P('dp', 'heads'), may hold values from -6 to 6
- lengths_seen: int32 [64, 4], P('dp', 'heads'), may hold values from 1025 to 2048, as said below
- page_table: int32 [64, 8], P('dp'), may hold values from 0 to 63, as said below
- finished: int32 [64], P('dp'), may hold values from 0 to 1, as said below
- move_plan: int32 [256, 3], P('dp'), may hold values from 0 to 63, as said below
Outputs:
- attention: bfloat16 [64, 16, 128], P('dp', 'heads')
Inputs may be any that keep to these rules, and one draw needn't show every extreme that they name: `lengths_seen`: each session's length, the largest entry of its row, lies between (5) * 256 + 1 and 2048. `page_table`: the 8 rows of one device's sessions hold each of that device's slot numbers exactly once. At most 2 sessions of one device are finished. `move_plan`: A row's source device differs from its receiving device; the destination slots of one receiving device are distinct, and each holds, after the moves, a page below the length of a session that is not finished. One device receives at most 5 pages from one source device, and on every device some source sends exactly 5.
All inputs are finite; a program needn't handle non-finite values.
Results may differ from a plain program's by a relative error of at most 0.008.
Values may be sent and summed in bfloat16 or wider, within the bound.
No kernel may reach another device: no remote copies, remote signals or barrier semaphores. Data moves between devices by JAX's collectives and lax.ppermute only.
A program may use at most 64 MiB of HBM per device.

v0:
```python
import functools
import math

import jax
import jax.numpy as jnp
from jax import lax
from jax.experimental import pallas as pl
from jax.experimental.pallas import tpu as pltpu
from jax.sharding import PartitionSpec as P

softcap_limit = 50.0
score_divisor = 12.0
exp_scale = softcap_limit * math.log2(math.e)
GROUP = 4
LEN_BASE = 128
SMALL_VMEM = 4 << 20
SESS_LANE, PAGE_LANE, HIGH_LANE, LOW_LANE = 32, 64, 96, 112

VMEM = pl.BlockSpec(memory_space=pltpu.VMEM)
HBM = pl.BlockSpec(memory_space=pltpu.HBM)


def in_hbm(array):
    return pltpu.with_memory_space_constraint(array, pltpu.HBM)


def load_all(pairs, sems):
    copies = [pltpu.make_async_copy(s, d, sems.at[i]) for i, (s, d) in enumerate(pairs)]
    for copy in copies:
        copy.start()
    return copies


def pack_kernel(
    n_heads, len_hbm, table_hbm, plan_hbm, query_hbm, out_ref,
    len_ref, table_ref, plan_ref, query_ref, sems, owner, count, meta,
):
    copies = load_all(
        [(len_hbm, len_ref), (table_hbm, table_ref), (plan_hbm, plan_ref), (query_hbm, query_ref)],
        sems,
    )
    sessions, pages_max = table_ref.shape
    moves = plan_ref.shape[1]
    devices, tiles = out_ref.shape[:2]
    n_dp = devices // n_heads
    rows = out_ref.shape[2]
    head = lax.axis_index("heads")
    lane = lax.broadcasted_iota(jnp.int32, (1, 128), 1)
    base = jnp.zeros((1, 128), jnp.int32)
    for d in range(n_dp):
        count[d] = 0
    for copy in copies:
        copy.wait()
    for s in range(sessions):
        length = len_ref[0, s]
        base = jnp.where(lane == HIGH_LANE + s, length // LEN_BASE, base)
        base = jnp.where(lane == LOW_LANE + s, length % LEN_BASE, base)
        for p in range(pages_max):
            owner[table_ref[s, p]] = s * 256 + p
    for d in range(n_dp):
        meta[d] = base
    for r in range(moves):
        source = plan_ref[0, r]
        rank = count[source]
        count[source] = rank + 1
        entry = owner[plan_ref[2, r]]
        session = entry >> 8
        row = meta[source]
        row = jnp.where(lane == rank, plan_ref[1, r] + 1, row)
        row = jnp.where(lane == SESS_LANE + rank, session, row)
        row = jnp.where(lane == PAGE_LANE + rank, entry & 255, row)
        meta[source] = row
        out_ref[source * n_heads + head, rank] = query_ref[session]
    for d in range(n_dp):
        row = jnp.broadcast_to(meta[d].astype(jnp.float32), (rows, 128)).astype(jnp.bfloat16)
        for h in range(n_heads):
            out_ref[d * n_heads + h, tiles - 1] = row


def decode(recv_ref, index):
    tile = recv_ref[index, recv_ref.shape[1] - 1]
    return tile.astype(jnp.float32).astype(jnp.int32)[0:1]


def longest_of(recv_ref, d, n_heads):
    longest = None
    for h in range(n_heads):
        block = decode(recv_ref, d * n_heads + h)
        length = block * LEN_BASE + pltpu.roll(block, 128 - (LOW_LANE - HIGH_LANE), 1)
        longest = length if longest is None else jnp.maximum(longest, length)
    return longest


class Pages:
    def __init__(self, key_hbm, value_hbm, entries, key_buf, value_buf, sems, num, den):
        self.key_hbm, self.value_hbm, self.entries = key_hbm, value_hbm, entries
        self.key_buf, self.value_buf, self.sems = key_buf, value_buf, sems
        self.num, self.den = num, den
        self.kv_heads, self.page_size = key_hbm.shape[1:3]
        self.rows = num.shape[1]
        self.group = self.rows // self.kv_heads

    def start(self, i, slot):
        pltpu.make_async_copy(
            self.key_hbm.at[slot], self.key_buf.at[i], self.sems.at[0, i]
        ).start()
        pltpu.make_async_copy(
            self.value_hbm.at[slot], self.value_buf.at[i], self.sems.at[1, i]
        ).start()

    def add(self, total, needed, slot, live, row, query):
        @pl.when(needed)
        def _():
            self.start(total, slot)
            self.entries[0, total] = total
            self.entries[1, total] = live
            self.entries[2, total] = row
            self.entries[3, total] = query

        return total + needed.astype(jnp.int32)

    def wait(self, first, total, which):
        buf, hbm = (self.key_buf, self.key_hbm) if which == 0 else (self.value_buf, self.value_hbm)
        for j in range(GROUP):
            i = first + j

            @pl.when(i < total)
            def _(i=i):
                pltpu.make_async_copy(hbm.at[0], buf.at[i], self.sems.at[which, i]).wait()

    def scores(self, first, get_query):
        raws = []
        for j in range(GROUP):
            i = first + j
            query = get_query(self.entries[3, i])
            buffer = self.entries[0, i]
            raws.append(
                [
                    lax.dot_general(
                        query,
                        self.key_buf[buffer, k],
                        (((1,), (1,)), ((), ())),
                        preferred_element_type=jnp.float32,
                    )
                    for k in range(self.kv_heads)
                ]
            )
        return raws

    def select(self, parts):
        row = lax.broadcasted_iota(jnp.int32, parts[0].shape, 0)
        out = parts[-1]
        for k in reversed(range(self.kv_heads - 1)):
            out = jnp.where(row < (k + 1) * self.group, parts[k], out)
        return out

    def weights(self, first, raws):
        out = []
        place = lax.broadcasted_iota(jnp.int32, (self.rows, self.page_size), 1)
        for j in range(GROUP):
            raw = self.select(raws[j])
            capped = jnp.tanh(raw * (1.0 / (score_divisor * softcap_limit)))
            weight = jnp.exp2(capped * exp_scale)
            live = self.entries[1, first + j]
            out.append(jnp.where(place < live, weight, 0.0).astype(jnp.bfloat16))
        return out

    def products(self, first, weights):
        parts = []
        for j in range(GROUP):
            buffer = self.entries[0, first + j]
            parts.append(
                [
                    jnp.dot(
                        weights[j], self.value_buf[buffer, k], preferred_element_type=jnp.float32
                    )
                    for k in range(self.kv_heads)
                ]
            )
        return parts

    def accumulate(self, first, weights, parts):
        for j in range(GROUP):
            row = self.entries[2, first + j]
            total = jnp.sum(weights[j].astype(jnp.float32), axis=1, keepdims=True)
            out = self.select(parts[j])
            self.num[row] = self.num[row] + out
            self.den[row] = self.den[row] + jnp.broadcast_to(total, out.shape)

    def run(self, total, get_query):
        for j in range(GROUP):
            for field in range(4):
                self.entries[field, total + j] = 0

        @pl.when(total == 0)
        def _():
            self.start(0, 0)

        total = jnp.maximum(total, 1)
        groups = (total + GROUP - 1) // GROUP
        self.wait(0, total, 0)
        weights = self.weights(0, self.scores(0, get_query))

        def step(g, weights):
            first = g * GROUP
            before = first - GROUP
            self.wait(first, total, 0)
            self.wait(before, total, 1)
            raws = self.scores(first, get_query)
            parts = self.products(before, weights)
            later = self.weights(first, raws)
            self.accumulate(before, weights, parts)
            return later

        weights = lax.fori_loop(1, groups, step, weights)
        last = (groups - 1) * GROUP
        self.wait(last, total, 1)
        self.accumulate(last, weights, self.products(last, weights))


def remote_kernel(
    n_heads, recv_ref, key_hbm, value_hbm, out_ref,
    meta, scalars, copied, num, den, entries, key_buf, value_buf, sems,
):
    devices, tiles, rows = recv_ref.shape[:3]
    n_dp = devices // n_heads
    capacity = tiles - 1
    sessions = out_ref.shape[1] - 1
    page_size = key_hbm.shape[2]
    head = lax.axis_index("heads")
    lane = lax.broadcasted_iota(jnp.int32, (1, 128), 1)
    for d in range(n_dp):
        own = decode(recv_ref, d * n_heads + head)
        meta[d : d + 1, :] = jnp.where(
            lane >= HIGH_LANE, longest_of(recv_ref, d, n_heads), own
        )
    copy = pltpu.make_async_copy(meta, scalars, copied)
    copy.start()
    num[...] = jnp.zeros_like(num)
    den[...] = jnp.zeros_like(den)
    queries_ref = recv_ref.reshape(devices * tiles, rows, recv_ref.shape[3])
    copy.wait()

    pages = Pages(key_hbm, value_hbm, entries, key_buf, value_buf, sems, num, den)
    total = jnp.int32(0)
    for d in range(n_dp):
        for c in range(capacity):
            slot = scalars[d, c]
            session = scalars[d, SESS_LANE + c]
            page = scalars[d, PAGE_LANE + c]
            live = jnp.clip(scalars[d, HIGH_LANE + session] - page * page_size, 0, page_size)
            total = pages.add(
                total,
                slot > 0,
                slot - 1,
                live,
                d * sessions + session,
                (d * n_heads + head) * tiles + c,
            )
    pages.run(total, lambda tile: queries_ref[tile])

    tile_lane = lax.broadcasted_iota(jnp.int32, (rows, 128), 1)
    for d in range(n_dp):
        packed = jnp.zeros((rows, 128), jnp.float32)
        for s in range(sessions):
            out_ref[d, s] = num[d * sessions + s].astype(jnp.bfloat16)
            value = den[d * sessions + s]
            high = value.astype(jnp.bfloat16).astype(jnp.float32)
            packed = jnp.where(tile_lane == s, high, packed)
            packed = jnp.where(tile_lane == 64 + s, value - high, packed)
        out_ref[d, sessions] = packed.astype(jnp.bfloat16)


def local_kernel(
    n_heads, recv_ref, table_hbm, plan_hbm, finished_hbm, query_hbm, key_hbm, value_hbm,
    num, den, table_ref, plan_ref, finished_ref, query_ref, loads, meta, scalars, copied,
    moved, entries, key_buf, value_buf, sems,
):
    copies = load_all(
        [
            (table_hbm, table_ref),
            (plan_hbm, plan_ref),
            (finished_hbm, finished_ref),
            (query_hbm, query_ref),
        ],
        loads,
    )
    sessions, pages_max = table_ref.shape
    page_size = key_hbm.shape[2]
    slots = key_hbm.shape[0]
    longest = longest_of(recv_ref, lax.axis_index("dp"), n_heads)
    meta[...] = jnp.broadcast_to(longest, meta.shape)
    copy = pltpu.make_async_copy(meta, scalars, copied)
    copy.start()
    num[...] = jnp.zeros_like(num)
    for j in range(slots):
        moved[j] = 0
    for load in copies:
        load.wait()
    for s in range(sessions):
        den[s] = jnp.full(den.shape[1:], 1.0, jnp.float32) * finished_ref[0, s].astype(jnp.float32)
    for r in range(plan_ref.shape[1]):
        moved[plan_ref[2, r]] = 1
    copy.wait()
    pages = Pages(key_hbm, value_hbm, entries, key_buf, value_buf, sems, num, den)
    total = jnp.int32(0)
    for s in range(sessions):
        length = jnp.where(finished_ref[0, s] == 1, 0, scalars[0, HIGH_LANE + s])
        for p in range(pages_max):
            slot = table_ref[s, p]
            live = jnp.clip(length - p * page_size, 0, page_size)
            needed = (live > 0) & (moved[slot] == 0)
            total = pages.add(total, needed, slot, live, s, s)
    pages.run(total, lambda session: query_ref[session])


def combine_kernel(back_ref, num_ref, den_ref, out_ref):
    n_dp, tiles, rows = back_ref.shape[:3]
    sessions = tiles - 1
    packed = back_ref[0, sessions].astype(jnp.float32)
    for d in range(1, n_dp):
        packed = packed + back_ref[d, sessions].astype(jnp.float32)
    packed = packed + pltpu.roll(packed, 64, 1)
    for s in range(sessions):
        total = num_ref[s]
        for d in range(n_dp):
            total = total + back_ref[d, s].astype(jnp.float32)
        weight = den_ref[s] + jnp.broadcast_to(packed[:, s : s + 1], (rows, 128))
        out_ref[s] = (total / weight).astype(jnp.bfloat16)


def body(queries, key_cache, value_cache, lengths_seen, page_table, finished, move_plan):
    slot_total, kv_heads, page_size, head_dim = key_cache.shape
    sessions, q_heads, _ = queries.shape
    pages_max = page_table.shape[1]
    moves = move_plan.shape[0]
    n_dp = lax.axis_size("dp")
    n_heads = lax.axis_size("heads")
    capacity = (moves - 1) // (n_dp - 1) + 1
    assert capacity <= 32 and sessions <= 16 and slot_total < 256 and pages_max <= 256

    seen = in_hbm(lengths_seen.T)
    plan = in_hbm(move_plan.T)
    table = in_hbm(page_table)
    query = in_hbm(queries)
    done = in_hbm(finished.reshape(1, sessions))
    keys = in_hbm(key_cache)
    values = in_hbm(value_cache)

    packed = pl.pallas_call(
        functools.partial(pack_kernel, n_heads),
        out_shape=jax.ShapeDtypeStruct(
            (n_dp * n_heads, capacity + 1, q_heads, head_dim), jnp.bfloat16
        ),
        in_specs=[HBM] * 4,
        out_specs=VMEM,
        scratch_shapes=[
            pltpu.SMEM((1, sessions), jnp.int32),
            pltpu.SMEM((sessions, pages_max), jnp.int32),
            pltpu.SMEM(plan.shape, jnp.int32),
            pltpu.VMEM(queries.shape, queries.dtype),
            pltpu.SemaphoreType.DMA((4,)),
            pltpu.SMEM((slot_total,), jnp.int32),
            pltpu.SMEM((n_dp,), jnp.int32),
            pltpu.VMEM((n_dp, 1, 128), jnp.int32),
        ],
        compiler_params=pltpu.CompilerParams(vmem_limit_bytes=SMALL_VMEM),
        name="pack",
    )(seen, table, plan, query)
    recv = lax.all_to_all(packed, ("dp", "heads"), split_axis=0, concat_axis=0, tiled=True)

    def page_scratch(count):
        buffer = pltpu.VMEM((count, kv_heads, page_size, head_dim), jnp.bfloat16)
        return [
            pltpu.SMEM((4, count + GROUP), jnp.int32),
            buffer,
            buffer,
            pltpu.SemaphoreType.DMA((2, count)),
        ]

    def page_limit(count):
        pages = 2 * count * kv_heads * page_size * head_dim * 2
        return pltpu.CompilerParams(vmem_limit_bytes=pages + SMALL_VMEM)

    asked = n_dp * capacity
    response = pl.pallas_call(
        functools.partial(remote_kernel, n_heads),
        out_shape=jax.ShapeDtypeStruct((n_dp, sessions + 1, q_heads, head_dim), jnp.bfloat16),
        in_specs=[VMEM, HBM, HBM],
        out_specs=VMEM,
        scratch_shapes=[
            pltpu.VMEM((n_dp, 128), jnp.int32),
            pltpu.SMEM((n_dp, 128), jnp.int32),
            pltpu.SemaphoreType.DMA,
            pltpu.VMEM((n_dp * sessions, q_heads, head_dim), jnp.float32),
            pltpu.VMEM((n_dp * sessions, q_heads, head_dim), jnp.float32),
            *page_scratch(asked),
        ],
        compiler_params=page_limit(asked),
        name="remote_pages",
        cost_estimate=pl.CostEstimate(flops=10**8, transcendentals=0, bytes_accessed=10**7),
    )(recv, keys, values)
    back = lax.all_to_all(response, "dp", split_axis=0, concat_axis=0, tiled=True)
    held = sessions * pages_max
    accumulator = jax.ShapeDtypeStruct((sessions, q_heads, head_dim), jnp.float32)
    num, den = pl.pallas_call(
        functools.partial(local_kernel, n_heads),
        out_shape=(accumulator, accumulator),
        in_specs=[VMEM, HBM, HBM, HBM, HBM, HBM, HBM],
        out_specs=(VMEM, VMEM),
        scratch_shapes=[
            pltpu.SMEM((sessions, pages_max), jnp.int32),
            pltpu.SMEM(plan.shape, jnp.int32),
            pltpu.SMEM((1, sessions), jnp.int32),
            pltpu.VMEM(queries.shape, queries.dtype),
            pltpu.SemaphoreType.DMA((4,)),
            pltpu.VMEM((8, 128), jnp.int32),
            pltpu.SMEM((8, 128), jnp.int32),
            pltpu.SemaphoreType.DMA,
            pltpu.SMEM((slot_total,), jnp.int32),
            *page_scratch(held),
        ],
        compiler_params=page_limit(held),
        name="local_pages",
        cost_estimate=pl.CostEstimate(flops=10**9, transcendentals=0, bytes_accessed=10**7),
    )(recv, table, plan, done, query, keys, values)
    return pl.pallas_call(
        combine_kernel,
        out_shape=jax.ShapeDtypeStruct((sessions, q_heads, head_dim), jnp.bfloat16),
        in_specs=[VMEM, VMEM, VMEM],
        out_specs=VMEM,
        compiler_params=pltpu.CompilerParams(vmem_limit_bytes=SMALL_VMEM),
        name="combine",
    )(back, num, den)


def solution(mesh):
    in_specs = (
        P("dp", "heads", None),
        P("dp", "heads", None, None),
        P("dp", "heads", None, None),
        P("dp", "heads"),
        P("dp", None),
        P("dp"),
        P("dp", None),
    )
    out_specs = P("dp", "heads", None)
    return jax.shard_map(body, mesh=mesh, in_specs=in_specs, out_specs=out_specs, check_vma=False)
```

profile of v0, /device:TPU:0, one launch (start us, length us, event | category | flops | bytes accessed | tf_op | source)
XLA Modules:
  0.0 35.6 jit_solution(3100699346831766410)
XLA Ops:
  0.0 1.1 %pack.1 = bf16[32,6,4,128]{3,2,1,0:T(4,128)(2,1)S(1)} custom-call(s32[1,8]{1,0:T(1,128)} %bitcast.5, s32[8,8]{1,0:T(8,128)} %table_hbm.3, s32[3,32]{1,0:T(4,128)} %bitcast.3, bf16[8,4,128]{2,1,0:T(4,128)(2,1)} %query_hbm.3), custom_call_target="tpu_custom_call" | custom-call | tf_op jit(solution)/shard_map/pack/pallas_call | solution.py:350
  1.1 16.1 %all_to_all.10.recv_ref = bf16[32,6,4,128]{3,2,1,0:T(4,128)(2,1)S(1)} all-to-all(bf16[32,6,4,128]{3,2,1,0:T(4,128)(2,1)S(1)} %pack.1), channel_id=1, replica_groups=mesh['dp'=8,'heads'=4] {'dp','heads'}, dimensions={0} | all-to-all | bytes 393216 | tf_op jit(solution)/shard_map/all_to_all | solution.py:370
  17.2 7.2 %remote_pages.1 = bf16[8,9,4,128]{3,2,1,0:T(4,128)(2,1)} custom-call(bf16[32,6,4,128]{3,2,1,0:T(4,128)(2,1)S(1)} %all_to_all.10.recv_ref, bf16[64,2,256,128]{3,2,1,0:T(8,128)(2,1)} %key_hbm.3, bf16[64,2,256,128]{3,2,1,0:T(8,128)(2,1)} %value_hbm.3), custom_call_target="tpu_custom_call" | custom-call | flops 100000000 | bytes 10000000 | tf_op jit(solution)/shard_map/remote_pages/pallas_call | solution.py:386
  24.4 3.4 %all-to-all-start.1 = ((bf16[8,9,4,128]{3,2,1,0:T(4,128)(2,1)}), bf16[8,9,4,128]{3,2,1,0:T(4,128)(2,1)S(1)}, u32[]{:S(2)}, u32[]{:S(2)}) async-start(bf16[8,9,4,128]{3,2,1,0:T(4,128)(2,1)} %remote_pages.1), calls=%async_computation.1 | async-start | bytes 147456 | tf_op jit(solution)/shard_map/all_to_all | solution.py:403
  27.8 4.8 %local_pages.1 = (f32[8,4,128]{2,1,0:T(4,128)S(1)}, f32[8,4,128]{2,1,0:T(4,128)S(1)}) custom-call(bf16[32,6,4,128]{3,2,1,0:T(4,128)(2,1)S(1)} %all_to_all.10.recv_ref, s32[8,8]{1,0:T(8,128)} %table_hbm.3, s32[3,32]{1,0:T(4,128)} %bitcast.4, s32[1,8]{1,0:T(1,128)} %bitcast.6, bf16[8,4,128]{2,1,0:T(4,128)(2,1)} %query_hbm.3, ...), custom_call_target="tpu_custom_call" | custom-call | flops 1000000000 | bytes 10000000 | tf_op jit(solution)/shard_map/local_pages/pallas_call | solution.py:406
  32.6 2.2 %all-to-all-done.1.back_ref = bf16[8,9,4,128]{3,2,1,0:T(4,128)(2,1)S(1)} async-done(((bf16[8,9,4,128]{3,2,1,0:T(4,128)(2,1)}), bf16[8,9,4,128]{3,2,1,0:T(4,128)(2,1)S(1)}, u32[]{:S(2)}, u32[]{:S(2)}) %all-to-all-start.1) | async-done | bytes 73760 | tf_op jit(solution)/shard_map/all_to_all | solution.py:403
  34.8 0.8 %combine.1 = bf16[8,4,128]{2,1,0:T(4,128)(2,1)} custom-call(bf16[8,9,4,128]{3,2,1,0:T(4,128)(2,1)S(1)} %all-to-all-done.1.back_ref, f32[8,4,128]{2,1,0:T(4,128)S(1)} %get-tuple-element.7.num_ref, f32[8,4,128]{2,1,0:T(4,128)S(1)} %get-tuple-element.8.den_ref), custom_call_target="tpu_custom_call" | custom-call | tf_op jit(solution)/shard_map/combine/pallas_call | solution.py:427
Async XLA Ops:
  24.4 10.4 %all-to-all-start.1 = ((bf16[8,9,4,128]{3,2,1,0:T(4,128)(2,1)}), bf16[8,9,4,128]{3,2,1,0:T(4,128)(2,1)S(1)}, u32[]{:S(2)}, u32[]{:S(2)}) async-start(bf16[8,9,4,128]{3,2,1,0:T(4,128)(2,1)} %remote_pages.1), calls=%async_computation.1 | async-start | bytes 147456 | tf_op jit(solution)/shard_map/all_to_all | solution.py:403
where the time goes:
time: 35.6 us
  blocking collectives  16.1 us (45%)
  Pallas kernels  13.9 us (39%)
  starting transfers between devices  3.36 us (9%)
  waiting for transfers between devices  2.2 us (6%)
    all_to_all x1, blocking collectives, body(): lax.all_to_all(packed, ('dp', 'heads'), split_axis=0, concat_axis=0, tile...  16.1 us
    pallas_call x1, Pallas kernels, body(): pl.pallas_call(functools.partial(remote_kernel, n_heads), out_shape=jax.S...  7.19 us
    pallas_call x1, Pallas kernels, body(): pl.pallas_call(functools.partial(local_kernel, n_heads), out_shape=(accum...  4.81 us
    all_to_all x1, starting transfers between devices, body(): lax.all_to_all(response, 'dp', split_axis=0, concat_axis=0, tiled=True)  3.36 us
    all_to_all x1, waiting for transfers between devices, body(): lax.all_to_all(response, 'dp', split_axis=0, concat_axis=0, tiled=True)  2.2 us
    pallas_call x1, Pallas kernels, body(): pl.pallas_call(functools.partial(pack_kernel, n_heads), out_shape=jax.Sha...  1.11 us
    pallas_call x1, Pallas kernels, body(): pl.pallas_call(combine_kernel, out_shape=jax.ShapeDtypeStruct((sessions,...  0.76 us
  transfers between devices with their start and end apart: 1, of which 1 were waited for; matrix products, arithmetic and copies ran while one was open for 0% of the time, Pallas kernels for 14%

commit v1 on v0

--- a/solution.py
+++ b/solution.py
@@ -11,7 +11,7 @@
 softcap_limit = 50.0
 score_divisor = 12.0
 exp_scale = softcap_limit * math.log2(math.e)
-GROUP = 4
+GROUP = 5
 LEN_BASE = 128
 SMALL_VMEM = 4 << 20
 SESS_LANE, PAGE_LANE, HIGH_LANE, LOW_LANE = 32, 64, 96, 112
@@ -92,39 +92,54 @@
 
 
 class Pages:
-    def __init__(self, key_hbm, value_hbm, entries, key_buf, value_buf, sems, num, den):
-        self.key_hbm, self.value_hbm, self.entries = key_hbm, value_hbm, entries
+    def __init__(self, key_hbm, value_hbm, words, key_buf, value_buf, sems, num, den):
+        self.key_hbm, self.value_hbm, self.words = key_hbm, value_hbm, words
         self.key_buf, self.value_buf, self.sems = key_buf, value_buf, sems
         self.num, self.den = num, den
         self.kv_heads, self.page_size = key_hbm.shape[1:3]
         self.rows = num.shape[1]
         self.group = self.rows // self.kv_heads
-
-    def start(self, i, slot):
-        pltpu.make_async_copy(
-            self.key_hbm.at[slot], self.key_buf.at[i], self.sems.at[0, i]
-        ).start()
-        pltpu.make_async_copy(
-            self.value_hbm.at[slot], self.value_buf.at[i], self.sems.at[1, i]
-        ).start()
-
-    def add(self, total, needed, slot, live, row, query):
+        self.live_shift = key_hbm.shape[0].bit_length()
+        self.row_shift = self.live_shift + self.page_size.bit_length()
+
+    def word(self, slot, live, row):
+        return (slot + 1) + live * (1 << self.live_shift) + row * (1 << self.row_shift)
+
+    def slot(self, word):
+        return (word & ((1 << self.live_shift) - 1)) - 1
+
+    def live(self, i):
+        return (self.words[i] >> self.live_shift) & (2 * self.page_size - 1)
+
+    def row(self, i):
+        return self.words[i] >> self.row_shift
+
+    def buffer(self, i):
+        return jnp.minimum(i, self.total - 1)
+
+    def start(self, i, slot, which):
+        buf, hbm = (self.key_buf, self.key_hbm) if which == 0 else (self.value_buf, self.value_hbm)
+        pltpu.make_async_copy(hbm.at[slot], buf.at[i], self.sems.at[which, i]).start()
+
+    def add(self, total, needed, word):
         @pl.when(needed)
         def _():
-            self.start(total, slot)
-            self.entries[0, total] = total
-            self.entries[1, total] = live
-            self.entries[2, total] = row
-            self.entries[3, total] = query
+            self.start(total, self.slot(word), 0)
+            self.words[total] = word
+
+        @pl.when(needed & (total >= GROUP))
+        def _():
+            before = total - GROUP
+            self.start(before, self.slot(self.words[before]), 1)
 
         return total + needed.astype(jnp.int32)
 
-    def wait(self, first, total, which):
+    def wait(self, first, which):
         buf, hbm = (self.key_buf, self.key_hbm) if which == 0 else (self.value_buf, self.value_hbm)
         for j in range(GROUP):
             i = first + j
 
-            @pl.when(i < total)
+            @pl.when(i < self.total)
             def _(i=i):
                 pltpu.make_async_copy(hbm.at[0], buf.at[i], self.sems.at[which, i]).wait()
 
@@ -132,8 +147,8 @@
         raws = []
         for j in range(GROUP):
             i = first + j
-            query = get_query(self.entries[3, i])
-            buffer = self.entries[0, i]
+            query = get_query(i)
+            buffer = self.buffer(i)
             raws.append(
                 [
                     lax.dot_general(
@@ -161,14 +176,14 @@
             raw = self.select(raws[j])
             capped = jnp.tanh(raw * (1.0 / (score_divisor * softcap_limit)))
             weight = jnp.exp2(capped * exp_scale)
-            live = self.entries[1, first + j]
+            live = self.live(first + j)
             out.append(jnp.where(place < live, weight, 0.0).astype(jnp.bfloat16))
         return out
 
     def products(self, first, weights):
         parts = []
         for j in range(GROUP):
-            buffer = self.entries[0, first + j]
+            buffer = self.buffer(first + j)
             parts.append(
                 [
                     jnp.dot(
@@ -181,7 +196,7 @@
 
     def accumulate(self, first, weights, parts):
         for j in range(GROUP):
-            row = self.entries[2, first + j]
+            row = self.row(first + j)
             total = jnp.sum(weights[j].astype(jnp.float32), axis=1, keepdims=True)
             out = self.select(parts[j])
             self.num[row] = self.num[row] + out
@@ -189,23 +204,30 @@
 
     def run(self, total, get_query):
         for j in range(GROUP):
-            for field in range(4):
-                self.entries[field, total + j] = 0
+            self.words[total + j] = 0
 
         @pl.when(total == 0)
         def _():
-            self.start(0, 0)
+            self.start(0, 0, 0)
+            self.words[0] = self.word(0, 0, 0)
 
         total = jnp.maximum(total, 1)
+        self.total = total
+
+        def rest(i, carry):
+            self.start(i, self.slot(self.words[i]), 1)
+            return carry
+
+        lax.fori_loop(jnp.maximum(total - GROUP, 0), total, rest, 0)
         groups = (total + GROUP - 1) // GROUP
-        self.wait(0, total, 0)
+        self.wait(0, 0)
         weights = self.weights(0, self.scores(0, get_query))
 
         def step(g, weights):
             first = g * GROUP
             before = first - GROUP
-            self.wait(first, total, 0)
-            self.wait(before, total, 1)
+            self.wait(first, 0)
+            self.wait(before, 1)
             raws = self.scores(first, get_query)
             parts = self.products(before, weights)
             later = self.weights(first, raws)
@@ -214,13 +236,13 @@
 
         weights = lax.fori_loop(1, groups, step, weights)
         last = (groups - 1) * GROUP
-        self.wait(last, total, 1)
+        self.wait(last, 1)
         self.accumulate(last, weights, self.products(last, weights))
 
 
 def remote_kernel(
     n_heads, recv_ref, key_hbm, value_hbm, out_ref,
-    meta, scalars, copied, num, den, entries, key_buf, value_buf, sems,
+    meta, num, den, tiles_of, words, key_buf, value_buf, sems,
 ):
     devices, tiles, rows = recv_ref.shape[:3]
     n_dp = devices // n_heads
@@ -228,36 +250,33 @@
     sessions = out_ref.shape[1] - 1
     page_size = key_hbm.shape[2]
     head = lax.axis_index("heads")
-    lane = lax.broadcasted_iota(jnp.int32, (1, 128), 1)
-    for d in range(n_dp):
-        own = decode(recv_ref, d * n_heads + head)
-        meta[d : d + 1, :] = jnp.where(
-            lane >= HIGH_LANE, longest_of(recv_ref, d, n_heads), own
-        )
-    copy = pltpu.make_async_copy(meta, scalars, copied)
-    copy.start()
+    for d in range(n_dp):
+        meta[0, d : d + 1, :] = decode(recv_ref, d * n_heads + head)
+        meta[1, d : d + 1, :] = longest_of(recv_ref, d, n_heads)
+    own, longest = meta[0], meta[1]
+    session = pltpu.roll(own, 128 - SESS_LANE, 1)
+    page = pltpu.roll(own, 128 - PAGE_LANE, 1)
+    length = jnp.zeros_like(own)
+    for s in range(sessions):
+        known = jnp.broadcast_to(longest[:, HIGH_LANE + s : HIGH_LANE + s + 1], own.shape)
+        length = jnp.where(session == s, known, length)
+    live = jnp.clip(length - page * page_size, 0, page_size)
+    pages = Pages(key_hbm, value_hbm, words, key_buf, value_buf, sems, num, den)
+    device = lax.broadcasted_iota(jnp.int32, own.shape, 0)
+    asked = jnp.where(own > 0, pages.word(own - 1, live, device * sessions + session), 0)
     num[...] = jnp.zeros_like(num)
     den[...] = jnp.zeros_like(den)
     queries_ref = recv_ref.reshape(devices * tiles, rows, recv_ref.shape[3])
-    copy.wait()
-
-    pages = Pages(key_hbm, value_hbm, entries, key_buf, value_buf, sems, num, den)
+
     total = jnp.int32(0)
     for d in range(n_dp):
         for c in range(capacity):
-            slot = scalars[d, c]
-            session = scalars[d, SESS_LANE + c]
-            page = scalars[d, PAGE_LANE + c]
-            live = jnp.clip(scalars[d, HIGH_LANE + session] - page * page_size, 0, page_size)
-            total = pages.add(
-                total,
-                slot > 0,
-                slot - 1,
-                live,
-                d * sessions + session,
-                (d * n_heads + head) * tiles + c,
-            )
-    pages.run(total, lambda tile: queries_ref[tile])
+            word = asked[d, c]
+            tiles_of[total] = (d * n_heads + head) * tiles + c
+            total = pages.add(total, word > 0, word)
+    for j in range(GROUP):
+        tiles_of[total + j] = 0
+    pages.run(total, lambda i: queries_ref[tiles_of[i]])
 
     tile_lane = lax.broadcasted_iota(jnp.int32, (rows, 128), 1)
     for d in range(n_dp):
@@ -273,8 +292,8 @@
 
 def local_kernel(
     n_heads, recv_ref, table_hbm, plan_hbm, finished_hbm, query_hbm, key_hbm, value_hbm,
-    num, den, table_ref, plan_ref, finished_ref, query_ref, loads, meta, scalars, copied,
-    moved, entries, key_buf, value_buf, sems,
+    num, den, table_ref, plan_ref, finished_ref, query_ref, loads,
+    moved, words, key_buf, value_buf, sems,
 ):
     copies = load_all(
         [
@@ -289,9 +308,6 @@
     page_size = key_hbm.shape[2]
     slots = key_hbm.shape[0]
     longest = longest_of(recv_ref, lax.axis_index("dp"), n_heads)
-    meta[...] = jnp.broadcast_to(longest, meta.shape)
-    copy = pltpu.make_async_copy(meta, scalars, copied)
-    copy.start()
     num[...] = jnp.zeros_like(num)
     for j in range(slots):
         moved[j] = 0
@@ -301,17 +317,16 @@
         den[s] = jnp.full(den.shape[1:], 1.0, jnp.float32) * finished_ref[0, s].astype(jnp.float32)
     for r in range(plan_ref.shape[1]):
         moved[plan_ref[2, r]] = 1
-    copy.wait()
-    pages = Pages(key_hbm, value_hbm, entries, key_buf, value_buf, sems, num, den)
+    pages = Pages(key_hbm, value_hbm, words, key_buf, value_buf, sems, num, den)
     total = jnp.int32(0)
     for s in range(sessions):
-        length = jnp.where(finished_ref[0, s] == 1, 0, scalars[0, HIGH_LANE + s])
+        length = jnp.where(finished_ref[0, s] == 1, 0, longest[0, HIGH_LANE + s])
         for p in range(pages_max):
             slot = table_ref[s, p]
             live = jnp.clip(length - p * page_size, 0, page_size)
             needed = (live > 0) & (moved[slot] == 0)
-            total = pages.add(total, needed, slot, live, s, s)
-    pages.run(total, lambda session: query_ref[session])
+            total = pages.add(total, needed, pages.word(slot, live, s))
+    pages.run(total, lambda i: query_ref[pages.row(i)])
 
 
 def combine_kernel(back_ref, num_ref, den_ref, out_ref):
@@ -338,6 +353,7 @@
     n_heads = lax.axis_size("heads")
     capacity = (moves - 1) // (n_dp - 1) + 1
     assert capacity <= 32 and sessions <= 16 and slot_total < 256 and pages_max <= 256
+    assert page_size & (page_size - 1) == 0 and n_dp * sessions << 8 << 10 < 2**31
 
     seen = in_hbm(lengths_seen.T)
     plan = in_hbm(move_plan.T)
@@ -372,7 +388,7 @@
     def page_scratch(count):
         buffer = pltpu.VMEM((count, kv_heads, page_size, head_dim), jnp.bfloat16)
         return [
-            pltpu.SMEM((4, count + GROUP), jnp.int32),
+            pltpu.SMEM((count + GROUP,), jnp.int32),
             buffer,
             buffer,
             pltpu.SemaphoreType.DMA((2, count)),
@@ -389,11 +405,10 @@
         in_specs=[VMEM, HBM, HBM],
         out_specs=VMEM,
         scratch_shapes=[
-            pltpu.VMEM((n_dp, 128), jnp.int32),
-            pltpu.SMEM((n_dp, 128), jnp.int32),
-            pltpu.SemaphoreType.DMA,
+            pltpu.VMEM((2, n_dp, 128), jnp.int32),
             pltpu.VMEM((n_dp * sessions, q_heads, head_dim), jnp.float32),
             pltpu.VMEM((n_dp * sessions, q_heads, head_dim), jnp.float32),
+            pltpu.SMEM((asked + GROUP,), jnp.int32),
             *page_scratch(asked),
         ],
         compiler_params=page_limit(asked),
@@ -414,9 +429,6 @@
             pltpu.SMEM((1, sessions), jnp.int32),
             pltpu.VMEM(queries.shape, queries.dtype),
             pltpu.SemaphoreType.DMA((4,)),
-            pltpu.VMEM((8, 128), jnp.int32),
-            pltpu.SMEM((8, 128), jnp.int32),
-            pltpu.SemaphoreType.DMA,
             pltpu.SMEM((slot_total,), jnp.int32),
             *page_scratch(held),
         ],

time: 35.6 us -> 35.2 us (0.989)
    pallas_call x1, Pallas kernels: 7.19 us -> 6.69 us  [body(): pl.pallas_call(functools.partial(remote_kernel, n_heads), out_shape=jax.S...]
  transfers between devices with their start and end apart: 1 -> 1, of which waited for: 1 -> 1; matrix products, arithmetic and copies ran while one was open for 0% -> 0% of each run, Pallas kernels for 14% -> 15%
where the time goes in v1:
time: 35.2 us; the launch traced here: 35.1 us
  blocking collectives  16.1 us (46%)
  Pallas kernels  13.7 us (39%)
  starting transfers between devices  3.36 us (10%)
  waiting for transfers between devices  1.91 us (5%)
    all_to_all x1, blocking collectives, body(): lax.all_to_all(packed, ('dp', 'heads'), split_axis=0, concat_axis=0, tile...  16.1 us
    pallas_call x1, Pallas kernels, body(): pl.pallas_call(functools.partial(remote_kernel, n_heads), out_shape=jax.S...  6.69 us
    pallas_call x1, Pallas kernels, body(): pl.pallas_call(functools.partial(local_kernel, n_heads), out_shape=(accum...  5.11 us
    all_to_all x1, starting transfers between devices, body(): lax.all_to_all(response, 'dp', split_axis=0, concat_axis=0, tiled=True)  3.36 us
    all_to_all x1, waiting for transfers between devices, body(): lax.all_to_all(response, 'dp', split_axis=0, concat_axis=0, tiled=True)  1.91 us
    pallas_call x1, Pallas kernels, body(): pl.pallas_call(functools.partial(pack_kernel, n_heads), out_shape=jax.Sha...  1.11 us
    pallas_call x1, Pallas kernels, body(): pl.pallas_call(combine_kernel, out_shape=jax.ShapeDtypeStruct((sessions,...  0.76 us
  transfers between devices with their start and end apart: 1, of which 1 were waited for; matrix products, arithmetic and copies ran while one was open for 0% of the time, Pallas kernels for 15%

profile of v1, /device:TPU:0, one launch (start us, length us, event | category | flops | bytes accessed | tf_op | source)
XLA Modules:
  0.0 35.1 jit_solution(11751654944245161710)
XLA Ops:
  0.0 1.1 %pack.1 = bf16[32,6,4,128]{3,2,1,0:T(4,128)(2,1)S(1)} custom-call(s32[1,8]{1,0:T(1,128)} %bitcast.5, s32[8,8]{1,0:T(8,128)} %table_hbm.3, s32[3,32]{1,0:T(4,128)} %bitcast.3, bf16[8,4,128]{2,1,0:T(4,128)(2,1)} %query_hbm.3), custom_call_target="tpu_custom_call" | custom-call | tf_op jit(solution)/shard_map/pack/pallas_call | solution.py:366
  1.1 16.1 %all_to_all.10.recv_ref = bf16[32,6,4,128]{3,2,1,0:T(4,128)(2,1)S(1)} all-to-all(bf16[32,6,4,128]{3,2,1,0:T(4,128)(2,1)S(1)} %pack.1), channel_id=1, replica_groups=mesh['dp'=8,'heads'=4] {'dp','heads'}, dimensions={0} | all-to-all | bytes 393216 | tf_op jit(solution)/shard_map/all_to_all | solution.py:386
  17.2 6.7 %remote_pages.1 = bf16[8,9,4,128]{3,2,1,0:T(4,128)(2,1)} custom-call(bf16[32,6,4,128]{3,2,1,0:T(4,128)(2,1)S(1)} %all_to_all.10.recv_ref, bf16[64,2,256,128]{3,2,1,0:T(8,128)(2,1)} %key_hbm.3, bf16[64,2,256,128]{3,2,1,0:T(8,128)(2,1)} %value_hbm.3), custom_call_target="tpu_custom_call" | custom-call | flops 100000000 | bytes 10000000 | tf_op jit(solution)/shard_map/remote_pages/pallas_call | solution.py:402
  23.9 3.4 %all-to-all-start.1 = ((bf16[8,9,4,128]{3,2,1,0:T(4,128)(2,1)}), bf16[8,9,4,128]{3,2,1,0:T(4,128)(2,1)S(1)}, u32[]{:S(2)}, u32[]{:S(2)}) async-start(bf16[8,9,4,128]{3,2,1,0:T(4,128)(2,1)} %remote_pages.1), calls=%async_computation.1 | async-start | bytes 147456 | tf_op jit(solution)/shard_map/all_to_all | solution.py:418
  27.3 5.1 %local_pages.1 = (f32[8,4,128]{2,1,0:T(4,128)S(1)}, f32[8,4,128]{2,1,0:T(4,128)S(1)}) custom-call(bf16[32,6,4,128]{3,2,1,0:T(4,128)(2,1)S(1)} %all_to_all.10.recv_ref, s32[8,8]{1,0:T(8,128)} %table_hbm.3, s32[3,32]{1,0:T(4,128)} %bitcast.4, s32[1,8]{1,0:T(1,128)} %bitcast.6, bf16[8,4,128]{2,1,0:T(4,128)(2,1)} %query_hbm.3, ...), custom_call_target="tpu_custom_call" | custom-call | flops 1000000000 | bytes 10000000 | tf_op jit(solution)/shard_map/local_pages/pallas_call | solution.py:421
  32.4 1.9 %all-to-all-done.1.back_ref = bf16[8,9,4,128]{3,2,1,0:T(4,128)(2,1)S(1)} async-done(((bf16[8,9,4,128]{3,2,1,0:T(4,128)(2,1)}), bf16[8,9,4,128]{3,2,1,0:T(4,128)(2,1)S(1)}, u32[]{:S(2)}, u32[]{:S(2)}) %all-to-all-start.1) | async-done | bytes 73760 | tf_op jit(solution)/shard_map/all_to_all | solution.py:418
  34.3 0.8 %combine.1 = bf16[8,4,128]{2,1,0:T(4,128)(2,1)} custom-call(bf16[8,9,4,128]{3,2,1,0:T(4,128)(2,1)S(1)} %all-to-all-done.1.back_ref, f32[8,4,128]{2,1,0:T(4,128)S(1)} %get-tuple-element.7.num_ref, f32[8,4,128]{2,1,0:T(4,128)S(1)} %get-tuple-element.8.den_ref), custom_call_target="tpu_custom_call" | custom-call | tf_op jit(solution)/shard_map/combine/pallas_call | solution.py:439
Async XLA Ops:
  23.9 10.4 %all-to-all-start.1 = ((bf16[8,9,4,128]{3,2,1,0:T(4,128)(2,1)}), bf16[8,9,4,128]{3,2,1,0:T(4,128)(2,1)S(1)}, u32[]{:S(2)}, u32[]{:S(2)}) async-start(bf16[8,9,4,128]{3,2,1,0:T(4,128)(2,1)} %remote_pages.1), calls=%async_computation.1 | async-start | bytes 147456 | tf_op jit(solution)/shard_map/all_to_all | solution.py:418

commit v2 on v1

--- a/solution.py
+++ b/solution.py
@@ -44,6 +44,7 @@
     devices, tiles = out_ref.shape[:2]
     n_dp = devices // n_heads
     rows = out_ref.shape[2]
+    parts = query_ref.shape[1] // rows
     head = lax.axis_index("heads")
     lane = lax.broadcasted_iota(jnp.int32, (1, 128), 1)
     base = jnp.zeros((1, 128), jnp.int32)
@@ -70,7 +71,9 @@
         row = jnp.where(lane == SESS_LANE + rank, session, row)
         row = jnp.where(lane == PAGE_LANE + rank, entry & 255, row)
         meta[source] = row
-        out_ref[source * n_heads + head, rank] = query_ref[session]
+        tile = query_ref[session]
+        for k in range(parts):
+            out_ref[source * n_heads + head, rank * parts + k] = tile[k * rows : (k + 1) * rows]
     for d in range(n_dp):
         row = jnp.broadcast_to(meta[d].astype(jnp.float32), (rows, 128)).astype(jnp.bfloat16)
         for h in range(n_heads):
@@ -92,10 +95,12 @@
 
 
 class Pages:
-    def __init__(self, key_hbm, value_hbm, words, key_buf, value_buf, sems, num, den):
+    def __init__(
+        self, key_hbm, value_hbm, words, key_buf, value_buf, sems, num, den, per_device=None
+    ):
         self.key_hbm, self.value_hbm, self.words = key_hbm, value_hbm, words
         self.key_buf, self.value_buf, self.sems = key_buf, value_buf, sems
-        self.num, self.den = num, den
+        self.num, self.den, self.per_device = num, den, per_device
         self.kv_heads, self.page_size = key_hbm.shape[1:3]
         self.rows = num.shape[1]
         self.group = self.rows // self.kv_heads
@@ -200,7 +205,12 @@
             total = jnp.sum(weights[j].astype(jnp.float32), axis=1, keepdims=True)
             out = self.select(parts[j])
             self.num[row] = self.num[row] + out
-            self.den[row] = self.den[row] + jnp.broadcast_to(total, out.shape)
+            total = jnp.broadcast_to(total, out.shape)
+            if self.per_device:
+                lane = lax.broadcasted_iota(jnp.int32, out.shape, 1)
+                total = jnp.where(lane == (row & (self.per_device - 1)), total, 0.0)
+                row = row >> (self.per_device.bit_length() - 1)
+            self.den[row] = self.den[row] + total
 
     def run(self, total, get_query):
         for j in range(GROUP):
@@ -242,11 +252,13 @@
 
 def remote_kernel(
     n_heads, recv_ref, key_hbm, value_hbm, out_ref,
-    meta, num, den, tiles_of, words, key_buf, value_buf, sems,
+    meta, num, den, queries, words, key_buf, value_buf, sems,
 ):
-    devices, tiles, rows = recv_ref.shape[:3]
+    devices, tiles, part_rows = recv_ref.shape[:3]
+    rows = out_ref.shape[2]
     n_dp = devices // n_heads
-    capacity = tiles - 1
+    parts = rows // part_rows
+    capacity = (tiles - 1) // parts
     sessions = out_ref.shape[1] - 1
     page_size = key_hbm.shape[2]
     head = lax.axis_index("heads")
@@ -261,33 +273,27 @@
         known = jnp.broadcast_to(longest[:, HIGH_LANE + s : HIGH_LANE + s + 1], own.shape)
         length = jnp.where(session == s, known, length)
     live = jnp.clip(length - page * page_size, 0, page_size)
-    pages = Pages(key_hbm, value_hbm, words, key_buf, value_buf, sems, num, den)
+    pages = Pages(key_hbm, value_hbm, words, key_buf, value_buf, sems, num, den, sessions)
     device = lax.broadcasted_iota(jnp.int32, own.shape, 0)
     asked = jnp.where(own > 0, pages.word(own - 1, live, device * sessions + session), 0)
+    total = jnp.int32(0)
+    for d in range(n_dp):
+        for c in range(capacity):
+            word = asked[d, c]
+            for k in range(parts):
+                queries[total, k * part_rows : (k + 1) * part_rows] = recv_ref[
+                    d * n_heads + head, c * parts + k
+                ]
+            total = pages.add(total, word > 0, word)
     num[...] = jnp.zeros_like(num)
     den[...] = jnp.zeros_like(den)
-    queries_ref = recv_ref.reshape(devices * tiles, rows, recv_ref.shape[3])
-
-    total = jnp.int32(0)
-    for d in range(n_dp):
-        for c in range(capacity):
-            word = asked[d, c]
-            tiles_of[total] = (d * n_heads + head) * tiles + c
-            total = pages.add(total, word > 0, word)
-    for j in range(GROUP):
-        tiles_of[total + j] = 0
-    pages.run(total, lambda i: queries_ref[tiles_of[i]])
-
-    tile_lane = lax.broadcasted_iota(jnp.int32, (rows, 128), 1)
-    for d in range(n_dp):
-        packed = jnp.zeros((rows, 128), jnp.float32)
+    pages.run(total, lambda i: queries[i])
+
+    for d in range(n_dp):
         for s in range(sessions):
             out_ref[d, s] = num[d * sessions + s].astype(jnp.bfloat16)
-            value = den[d * sessions + s]
-            high = value.astype(jnp.bfloat16).astype(jnp.float32)
-            packed = jnp.where(tile_lane == s, high, packed)
-            packed = jnp.where(tile_lane == 64 + s, value - high, packed)
-        out_ref[d, sessions] = packed.astype(jnp.bfloat16)
+        high = den[d].astype(jnp.bfloat16).astype(jnp.float32)
+        out_ref[d, sessions] = (high + pltpu.roll(den[d] - high, 64, 1)).astype(jnp.bfloat16)
 
 
 def local_kernel(
@@ -353,7 +359,8 @@
     n_heads = lax.axis_size("heads")
     capacity = (moves - 1) // (n_dp - 1) + 1
     assert capacity <= 32 and sessions <= 16 and slot_total < 256 and pages_max <= 256
-    assert page_size & (page_size - 1) == 0 and n_dp * sessions << 8 << 10 < 2**31
+    assert page_size & (page_size - 1) == 0 and sessions & (sessions - 1) == 0
+    assert n_dp * sessions << 8 << 10 < 2**31
 
     seen = in_hbm(lengths_seen.T)
     plan = in_hbm(move_plan.T)
@@ -366,7 +373,7 @@
     packed = pl.pallas_call(
         functools.partial(pack_kernel, n_heads),
         out_shape=jax.ShapeDtypeStruct(
-            (n_dp * n_heads, capacity + 1, q_heads, head_dim), jnp.bfloat16
+            (n_dp * n_heads, capacity * kv_heads + 1, q_heads // kv_heads, head_dim), jnp.bfloat16
         ),
         in_specs=[HBM] * 4,
         out_specs=VMEM,
@@ -407,8 +414,8 @@
         scratch_shapes=[
             pltpu.VMEM((2, n_dp, 128), jnp.int32),
             pltpu.VMEM((n_dp * sessions, q_heads, head_dim), jnp.float32),
-            pltpu.VMEM((n_dp * sessions, q_heads, head_dim), jnp.float32),
-            pltpu.SMEM((asked + GROUP,), jnp.int32),
+            pltpu.VMEM((n_dp, q_heads, head_dim), jnp.float32),
+            pltpu.VMEM((asked + GROUP, q_heads, head_dim), jnp.bfloat16),
             *page_scratch(asked),
         ],
         compiler_params=page_limit(asked),

time: 35.2 us -> 34.9 us (level)
  waiting for transfers between devices: 1.91 us -> 1.42 us
    all_to_all x1, waiting for transfers between devices: 1.91 us -> 1.42 us  [body(): lax.all_to_all(response, 'dp', split_axis=0, concat_axis=0, tiled=True)]
    pallas_call x1, Pallas kernels: 5.11 us -> 5.49 us  [body(): pl.pallas_call(functools.partial(local_kernel, n_heads), out_shape=(accum...]
  transfers between devices with their start and end apart: 1 -> 1, of which waited for: 1 -> 1; matrix products, arithmetic and copies ran while one was open for 0% -> 0% of each run, Pallas kernels for 15% -> 16%
where the time goes in v2:
time: 34.9 us; the launch traced here: 34.6 us
  blocking collectives  15.9 us (46%)
  Pallas kernels  13.9 us (40%)
  starting transfers between devices  3.36 us (10%)
  waiting for transfers between devices  1.42 us (4%)
    all_to_all x1, blocking collectives, body(): lax.all_to_all(packed, ('dp', 'heads'), split_axis=0, concat_axis=0, tile...  15.9 us
    pallas_call x1, Pallas kernels, body(): pl.pallas_call(functools.partial(remote_kernel, n_heads), out_shape=jax.S...  6.53 us
    pallas_call x1, Pallas kernels, body(): pl.pallas_call(functools.partial(local_kernel, n_heads), out_shape=(accum...  5.49 us
    all_to_all x1, starting transfers between devices, body(): lax.all_to_all(response, 'dp', split_axis=0, concat_axis=0, tiled=True)  3.36 us
    all_to_all x1, waiting for transfers between devices, body(): lax.all_to_all(response, 'dp', split_axis=0, concat_axis=0, tiled=True)  1.42 us
    pallas_call x1, Pallas kernels, body(): pl.pallas_call(functools.partial(pack_kernel, n_heads), out_shape=jax.Sha...  1.11 us
    pallas_call x1, Pallas kernels, body(): pl.pallas_call(combine_kernel, out_shape=jax.ShapeDtypeStruct((sessions,...  0.76 us
  transfers between devices with their start and end apart: 1, of which 1 were waited for; matrix products, arithmetic and copies ran while one was open for 0% of the time, Pallas kernels for 16%

profile of v2, /device:TPU:0, one launch (start us, length us, event | category | flops | bytes accessed | tf_op | source)
XLA Modules:
  0.0 34.6 jit_solution(17408839068001135662)
XLA Ops:
  0.0 1.1 %pack.1 = bf16[32,11,2,128]{3,2,1,0:T(2,128)(2,1)S(1)} custom-call(s32[1,8]{1,0:T(1,128)} %bitcast.6, s32[8,8]{1,0:T(8,128)} %table_hbm.3, s32[3,32]{1,0:T(4,128)} %bitcast.3, bf16[8,4,128]{2,1,0:T(4,128)(2,1)} %query_hbm.3), custom_call_target="tpu_custom_call" | custom-call | tf_op jit(solution)/shard_map/pack/pallas_call | solution.py:373
  1.1 15.9 %all_to_all.10.recv_ref = bf16[32,11,2,128]{3,2,1,0:T(2,128)(2,1)S(1)} all-to-all(bf16[32,11,2,128]{3,2,1,0:T(2,128)(2,1)S(1)} %pack.1), channel_id=1, replica_groups=mesh['dp'=8,'heads'=4] {'dp','heads'}, dimensions={0} | all-to-all | bytes 360448 | tf_op jit(solution)/shard_map/all_to_all | solution.py:393
  17.1 6.5 %remote_pages.1 = bf16[8,9,4,128]{3,2,1,0:T(4,128)(2,1)} custom-call(bf16[32,11,2,128]{3,2,1,0:T(2,128)(2,1)S(1)} %all_to_all.10.recv_ref, bf16[64,2,256,128]{3,2,1,0:T(8,128)(2,1)} %key_hbm.3, bf16[64,2,256,128]{3,2,1,0:T(8,128)(2,1)} %value_hbm.3), custom_call_target="tpu_custom_call" | custom-call | flops 100000000 | bytes 10000000 | tf_op jit(solution)/shard_map/remote_pages/pallas_call | solution.py:409
  23.6 3.4 %all-to-all-start.1 = ((bf16[8,9,4,128]{3,2,1,0:T(4,128)(2,1)}), bf16[8,9,4,128]{3,2,1,0:T(4,128)(2,1)S(1)}, u32[]{:S(2)}, u32[]{:S(2)}) async-start(bf16[8,9,4,128]{3,2,1,0:T(4,128)(2,1)} %remote_pages.1), calls=%async_computation.1 | async-start | bytes 147456 | tf_op jit(solution)/shard_map/all_to_all | solution.py:425
  27.0 5.5 %local_pages.1 = (f32[8,4,128]{2,1,0:T(4,128)S(1)}, f32[8,4,128]{2,1,0:T(4,128)S(1)}) custom-call(bf16[32,11,2,128]{3,2,1,0:T(2,128)(2,1)S(1)} %all_to_all.10.recv_ref, s32[8,8]{1,0:T(8,128)} %table_hbm.3, s32[3,32]{1,0:T(4,128)} %bitcast.4, s32[1,8]{1,0:T(1,128)} %bitcast.5, bf16[8,4,128]{2,1,0:T(4,128)(2,1)} %query_hbm.3, ...), custom_call_target="tpu_custom_call" | custom-call | flops 1000000000 | bytes 10000000 | tf_op jit(solution)/shard_map/local_pages/pallas_call | solution.py:428
  32.5 1.4 %all-to-all-done.1.back_ref = bf16[8,9,4,128]{3,2,1,0:T(4,128)(2,1)S(1)} async-done(((bf16[8,9,4,128]{3,2,1,0:T(4,128)(2,1)}), bf16[8,9,4,128]{3,2,1,0:T(4,128)(2,1)S(1)}, u32[]{:S(2)}, u32[]{:S(2)}) %all-to-all-start.1) | async-done | bytes 73760 | tf_op jit(solution)/shard_map/all_to_all | solution.py:425
  33.9 0.8 %combine.1 = bf16[8,4,128]{2,1,0:T(4,128)(2,1)} custom-call(bf16[8,9,4,128]{3,2,1,0:T(4,128)(2,1)S(1)} %all-to-all-done.1.back_ref, f32[8,4,128]{2,1,0:T(4,128)S(1)} %get-tuple-element.7.num_ref, f32[8,4,128]{2,1,0:T(4,128)S(1)} %get-tuple-element.8.den_ref), custom_call_target="tpu_custom_call" | custom-call | tf_op jit(solution)/shard_map/combine/pallas_call | solution.py:446
Async XLA Ops:
  23.6 10.3 %all-to-all-start.1 = ((bf16[8,9,4,128]{3,2,1,0:T(4,128)(2,1)}), bf16[8,9,4,128]{3,2,1,0:T(4,128)(2,1)S(1)}, u32[]{:S(2)}, u32[]{:S(2)}) async-start(bf16[8,9,4,128]{3,2,1,0:T(4,128)(2,1)} %remote_pages.1), calls=%async_computation.1 | async-start | bytes 147456 | tf_op jit(solution)/shard_map/all_to_all | solution.py:425

commit v3 on v2

--- a/solution.py
+++ b/solution.py
@@ -251,15 +251,15 @@
 
 
 def remote_kernel(
-    n_heads, recv_ref, key_hbm, value_hbm, out_ref,
+    n_heads, sessions, recv_ref, key_hbm, value_hbm, out_ref,
     meta, num, den, queries, words, key_buf, value_buf, sems,
 ):
     devices, tiles, part_rows = recv_ref.shape[:3]
-    rows = out_ref.shape[2]
+    rows = num.shape[1]
     n_dp = devices // n_heads
     parts = rows // part_rows
     capacity = (tiles - 1) // parts
-    sessions = out_ref.shape[1] - 1
+    places = num.shape[0] // n_dp
     page_size = key_hbm.shape[2]
     head = lax.axis_index("heads")
     for d in range(n_dp):
@@ -273,9 +273,10 @@
         known = jnp.broadcast_to(longest[:, HIGH_LANE + s : HIGH_LANE + s + 1], own.shape)
         length = jnp.where(session == s, known, length)
     live = jnp.clip(length - page * page_size, 0, page_size)
-    pages = Pages(key_hbm, value_hbm, words, key_buf, value_buf, sems, num, den, sessions)
+    pages = Pages(key_hbm, value_hbm, words, key_buf, value_buf, sems, num, den, places)
     device = lax.broadcasted_iota(jnp.int32, own.shape, 0)
-    asked = jnp.where(own > 0, pages.word(own - 1, live, device * sessions + session), 0)
+    place = lax.broadcasted_iota(jnp.int32, own.shape, 1) & (places - 1)
+    asked = jnp.where(own > 0, pages.word(own - 1, live, device * places + place), 0)
     total = jnp.int32(0)
     for d in range(n_dp):
         for c in range(capacity):
@@ -290,16 +291,21 @@
     pages.run(total, lambda i: queries[i])
 
     for d in range(n_dp):
-        for s in range(sessions):
-            out_ref[d, s] = num[d * sessions + s].astype(jnp.bfloat16)
+        for c in range(capacity):
+            out_ref[d, c * rows : (c + 1) * rows] = num[d * places + c].astype(jnp.bfloat16)
         high = den[d].astype(jnp.bfloat16).astype(jnp.float32)
-        out_ref[d, sessions] = (high + pltpu.roll(den[d] - high, 64, 1)).astype(jnp.bfloat16)
+        used = (capacity + 1) * rows
+        out_ref[d, used - rows : used] = (high + pltpu.roll(den[d] - high, 64, 1)).astype(
+            jnp.bfloat16
+        )
+        if used < out_ref.shape[1]:
+            out_ref[d, used:] = jnp.zeros((out_ref.shape[1] - used, 128), jnp.bfloat16)
 
 
 def local_kernel(
     n_heads, recv_ref, table_hbm, plan_hbm, finished_hbm, query_hbm, key_hbm, value_hbm,
-    num, den, table_ref, plan_ref, finished_ref, query_ref, loads,
-    moved, words, key_buf, value_buf, sems,
+    num, den, spread_ref, place_ref, table_ref, plan_ref, finished_ref, query_ref, loads,
+    moved, owner, count, words, key_buf, value_buf, sems,
 ):
     copies = load_all(
         [
@@ -334,19 +340,50 @@
             total = pages.add(total, needed, pages.word(slot, live, s))
     pages.run(total, lambda i: query_ref[pages.row(i)])
 
-
-def combine_kernel(back_ref, num_ref, den_ref, out_ref):
-    n_dp, tiles, rows = back_ref.shape[:3]
-    sessions = tiles - 1
-    packed = back_ref[0, sessions].astype(jnp.float32)
-    for d in range(1, n_dp):
-        packed = packed + back_ref[d, sessions].astype(jnp.float32)
-    packed = packed + pltpu.roll(packed, 64, 1)
+    n_dp = place_ref.shape[0]
+    rows = num.shape[1]
+    stride = spread_ref.shape[1] // n_dp
     for s in range(sessions):
-        total = num_ref[s]
+        for p in range(pages_max):
+            owner[table_ref[s, p]] = s
+    for d in range(n_dp):
+        count[d] = 0
+    row = lax.broadcasted_iota(jnp.int32, spread_ref.shape, 0)
+    column = lax.broadcasted_iota(jnp.int32, spread_ref.shape, 1)
+    device = lax.broadcasted_iota(jnp.int32, place_ref.shape, 0)
+    lane = lax.broadcasted_iota(jnp.int32, place_ref.shape, 1) & 63
+    session_row = row // rows
+    spread = jnp.zeros(spread_ref.shape, jnp.float32)
+    places = jnp.full(place_ref.shape, -1, jnp.int32)
+    for r in range(plan_ref.shape[1]):
+        source = plan_ref[0, r]
+        rank = count[source]
+        count[source] = rank + 1
+        session = owner[plan_ref[2, r]]
+        offset = source * stride + rank * rows - session * rows
+        spread = jnp.where((column - row == offset) & (session_row == session), 1.0, spread)
+        places = jnp.where((device == source) & (lane == rank), session, places)
+    spread_ref[...] = spread.astype(jnp.bfloat16)
+    place_ref[...] = places
+
+
+def combine_kernel(capacity, back_ref, num_ref, den_ref, spread_ref, place_ref, out_ref):
+    n_dp, stride = back_ref.shape[:2]
+    sessions, rows = num_ref.shape[:2]
+    moved = jnp.dot(
+        spread_ref[...],
+        back_ref[...].reshape(n_dp * stride, 128),
+        preferred_element_type=jnp.float32,
+    )
+    tile = slice(capacity * rows, (capacity + 1) * rows)
+    weights = [back_ref[d, tile].astype(jnp.float32) for d in range(n_dp)]
+    for s in range(sessions):
+        packed = jnp.zeros((rows, 128), jnp.float32)
         for d in range(n_dp):
-            total = total + back_ref[d, s].astype(jnp.float32)
-        weight = den_ref[s] + jnp.broadcast_to(packed[:, s : s + 1], (rows, 128))
+            mine = jnp.broadcast_to(place_ref[d : d + 1, :], (rows, 128)) == s
+            packed = packed + jnp.where(mine, weights[d], 0.0)
+        weight = den_ref[s] + jnp.sum(packed, axis=1, keepdims=True)
+        total = num_ref[s] + moved[s * rows : (s + 1) * rows]
         out_ref[s] = (total / weight).astype(jnp.bfloat16)
 
 
@@ -406,14 +443,16 @@
         return pltpu.CompilerParams(vmem_limit_bytes=pages + SMALL_VMEM)
 
     asked = n_dp * capacity
+    places = 1 << (capacity - 1).bit_length()
+    stride = -(-(capacity + 1) * q_heads // 8) * 8
     response = pl.pallas_call(
-        functools.partial(remote_kernel, n_heads),
-        out_shape=jax.ShapeDtypeStruct((n_dp, sessions + 1, q_heads, head_dim), jnp.bfloat16),
+        functools.partial(remote_kernel, n_heads, sessions),
+        out_shape=jax.ShapeDtypeStruct((n_dp, stride, head_dim), jnp.bfloat16),
         in_specs=[VMEM, HBM, HBM],
         out_specs=VMEM,
         scratch_shapes=[
             pltpu.VMEM((2, n_dp, 128), jnp.int32),
-            pltpu.VMEM((n_dp * sessions, q_heads, head_dim), jnp.float32),
+            pltpu.VMEM((n_dp * places, q_heads, head_dim), jnp.float32),
             pltpu.VMEM((n_dp, q_heads, head_dim), jnp.float32),
             pltpu.VMEM((asked + GROUP, q_heads, head_dim), jnp.bfloat16),
             *page_scratch(asked),
@@ -425,11 +464,16 @@
     back = lax.all_to_all(response, "dp", split_axis=0, concat_axis=0, tiled=True)
     held = sessions * pages_max
     accumulator = jax.ShapeDtypeStruct((sessions, q_heads, head_dim), jnp.float32)
-    num, den = pl.pallas_call(
+    num, den, spread, place = pl.pallas_call(
         functools.partial(local_kernel, n_heads),
-        out_shape=(accumulator, accumulator),
+        out_shape=(
+            accumulator,
+            accumulator,
+            jax.ShapeDtypeStruct((sessions * q_heads, n_dp * stride), jnp.bfloat16),
+            jax.ShapeDtypeStruct((n_dp, 128), jnp.int32),
+        ),
         in_specs=[VMEM, HBM, HBM, HBM, HBM, HBM, HBM],
-        out_specs=(VMEM, VMEM),
+        out_specs=(VMEM,) * 4,
         scratch_shapes=[
             pltpu.SMEM((sessions, pages_max), jnp.int32),
             pltpu.SMEM(plan.shape, jnp.int32),
@@ -437,6 +481,8 @@
             pltpu.VMEM(queries.shape, queries.dtype),
             pltpu.SemaphoreType.DMA((4,)),
             pltpu.SMEM((slot_total,), jnp.int32),
+            pltpu.SMEM((slot_total,), jnp.int32),
+            pltpu.SMEM((n_dp,), jnp.int32),
             *page_scratch(held),
         ],
         compiler_params=page_limit(held),
@@ -444,13 +490,13 @@
         cost_estimate=pl.CostEstimate(flops=10**9, transcendentals=0, bytes_accessed=10**7),
     )(recv, table, plan, done, query, keys, values)
     return pl.pallas_call(
-        combine_kernel,
+        functools.partial(combine_kernel, capacity),
         out_shape=jax.ShapeDtypeStruct((sessions, q_heads, head_dim), jnp.bfloat16),
-        in_specs=[VMEM, VMEM, VMEM],
+        in_specs=[VMEM] * 5,
         out_specs=VMEM,
         compiler_params=pltpu.CompilerParams(vmem_limit_bytes=SMALL_VMEM),
         name="combine",
-    )(back, num, den)
+    )(back, num, den, spread, place)
 
 
 def solution(mesh):

time: 34.9 us -> 34.8 us (level)
  transfers between devices with their start and end apart: 1 -> 1, of which waited for: 1 -> 1; matrix products, arithmetic and copies ran while one was open for 0% -> 0% of each run, Pallas kernels for 16% -> 15%
where the time goes in v3:
time: 34.8 us; the launch traced here: 34.5 us
  blocking collectives  15.9 us (46%)
  Pallas kernels  13.8 us (40%)
  starting transfers between devices  3.36 us (10%)
  waiting for transfers between devices  1.43 us (4%)
    all_to_all x1, blocking collectives, body(): lax.all_to_all(packed, ('dp', 'heads'), split_axis=0, concat_axis=0, tile...  15.9 us
    pallas_call x1, Pallas kernels, body(): pl.pallas_call(functools.partial(remote_kernel, n_heads, sessions), out_s...  6.61 us
    pallas_call x1, Pallas kernels, body(): pl.pallas_call(functools.partial(local_kernel, n_heads), out_shape=(accum...  5.29 us
    all_to_all x1, starting transfers between devices, body(): lax.all_to_all(response, 'dp', split_axis=0, concat_axis=0, tiled=True)  3.36 us
    all_to_all x1, waiting for transfers between devices, body(): lax.all_to_all(response, 'dp', split_axis=0, concat_axis=0, tiled=True)  1.43 us
    pallas_call x1, Pallas kernels, body(): pl.pallas_call(functools.partial(pack_kernel, n_heads), out_shape=jax.Sha...  1.11 us
    pallas_call x1, Pallas kernels, body(): pl.pallas_call(functools.partial(combine_kernel, capacity), out_shape=jax...  0.74 us
  transfers between devices with their start and end apart: 1, of which 1 were waited for; matrix products, arithmetic and copies ran while one was open for 0% of the time, Pallas kernels for 15%

profile of v3, /device:TPU:0, one launch (start us, length us, event | category | flops | bytes accessed | tf_op | source)
XLA Modules:
  0.0 34.5 jit_solution(10275344437018396517)
XLA Ops:
  0.0 1.1 %pack.1 = bf16[32,11,2,128]{3,2,1,0:T(2,128)(2,1)S(1)} custom-call(s32[1,8]{1,0:T(1,128)} %bitcast.6, s32[8,8]{1,0:T(8,128)} %table_hbm.3, s32[3,32]{1,0:T(4,128)} %bitcast.3, bf16[8,4,128]{2,1,0:T(4,128)(2,1)} %query_hbm.3), custom_call_target="tpu_custom_call" | custom-call | tf_op jit(solution)/shard_map/pack/pallas_call | solution.py:410
  1.1 15.9 %all_to_all.10.recv_ref = bf16[32,11,2,128]{3,2,1,0:T(2,128)(2,1)S(1)} all-to-all(bf16[32,11,2,128]{3,2,1,0:T(2,128)(2,1)S(1)} %pack.1), channel_id=1, replica_groups=mesh['dp'=8,'heads'=4] {'dp','heads'}, dimensions={0} | all-to-all | bytes 360448 | tf_op jit(solution)/shard_map/all_to_all | solution.py:430
  17.1 6.6 %remote_pages.1 = bf16[8,24,128]{2,1,0:T(8,128)(2,1)} custom-call(bf16[32,11,2,128]{3,2,1,0:T(2,128)(2,1)S(1)} %all_to_all.10.recv_ref, bf16[64,2,256,128]{3,2,1,0:T(8,128)(2,1)} %key_hbm.3, bf16[64,2,256,128]{3,2,1,0:T(8,128)(2,1)} %value_hbm.3), custom_call_target="tpu_custom_call" | custom-call | flops 100000000 | bytes 10000000 | tf_op jit(solution)/shard_map/remote_pages/pallas_call | solution.py:448
  23.7 3.4 %all-to-all-start.1 = ((bf16[8,24,128]{2,1,0:T(8,128)(2,1)}), bf16[8,24,128]{2,1,0:T(8,128)(2,1)S(1)}, u32[]{:S(2)}, u32[]{:S(2)}) async-start(bf16[8,24,128]{2,1,0:T(8,128)(2,1)} %remote_pages.1), calls=%async_computation.1 | async-start | bytes 98304 | tf_op jit(solution)/shard_map/all_to_all | solution.py:464
  27.0 5.3 %local_pages.1 = (f32[8,4,128]{2,1,0:T(4,128)S(1)}, f32[8,4,128]{2,1,0:T(4,128)S(1)}, bf16[32,192]{1,0:T(8,128)(2,1)S(1)}, s32[8,128]{1,0:T(8,128)S(1)}) custom-call(bf16[32,11,2,128]{3,2,1,0:T(2,128)(2,1)S(1)} %all_to_all.10.recv_ref, s32[8,8]{1,0:T(8,128)} %table_hbm.3, s32[3,32]{1,0:T(4,128)} %bitcast.4, s32[1,8]{1,0:T(1,128)} %bitcast.5, ...), custom_call_target="tpu_custom_call" | custom-call | flops 1000000000 | bytes 10000000 | tf_op jit(solution)/shard_map/local_pages/pallas_call | solution.py:467
  32.3 1.4 %all-to-all-done.1.back_ref = bf16[8,24,128]{2,1,0:T(8,128)(2,1)S(1)} async-done(((bf16[8,24,128]{2,1,0:T(8,128)(2,1)}), bf16[8,24,128]{2,1,0:T(8,128)(2,1)S(1)}, u32[]{:S(2)}, u32[]{:S(2)}) %all-to-all-start.1) | async-done | bytes 49184 | tf_op jit(solution)/shard_map/all_to_all | solution.py:464
  33.8 0.7 %combine.1 = bf16[8,4,128]{2,1,0:T(4,128)(2,1)} custom-call(bf16[8,24,128]{2,1,0:T(8,128)(2,1)S(1)} %all-to-all-done.1.back_ref, f32[8,4,128]{2,1,0:T(4,128)S(1)} %get-tuple-element.9.num_ref, f32[8,4,128]{2,1,0:T(4,128)S(1)} %get-tuple-element.10.den_ref, bf16[32,192]{1,0:T(8,128)(2,1)S(1)} %get-tuple-element.11.spread_ref, ...), custom_call_target="tpu_custom_call" | custom-call | tf_op jit(solution)/shard_map/combine/pallas_call | solution.py:492
Async XLA Ops:
  23.7 10.1 %all-to-all-start.1 = ((bf16[8,24,128]{2,1,0:T(8,128)(2,1)}), bf16[8,24,128]{2,1,0:T(8,128)(2,1)S(1)}, u32[]{:S(2)}, u32[]{:S(2)}) async-start(bf16[8,24,128]{2,1,0:T(8,128)(2,1)} %remote_pages.1), calls=%async_computation.1 | async-start | bytes 98304 | tf_op jit(solution)/shard_map/all_to_all | solution.py:464

commit v4 on v3

--- a/solution.py
+++ b/solution.py
@@ -96,11 +96,12 @@
 
 class Pages:
     def __init__(
-        self, key_hbm, value_hbm, words, key_buf, value_buf, sems, num, den, per_device=None
+        self, key_hbm, value_hbm, words, key_buf, value_buf, sems, num, den, per_device=None,
+        lives=None,
     ):
         self.key_hbm, self.value_hbm, self.words = key_hbm, value_hbm, words
         self.key_buf, self.value_buf, self.sems = key_buf, value_buf, sems
-        self.num, self.den, self.per_device = num, den, per_device
+        self.num, self.den, self.per_device, self.lives = num, den, per_device, lives
         self.kv_heads, self.page_size = key_hbm.shape[1:3]
         self.rows = num.shape[1]
         self.group = self.rows // self.kv_heads
@@ -114,6 +115,8 @@
         return (word & ((1 << self.live_shift) - 1)) - 1
 
     def live(self, i):
+        if self.lives is not None:
+            return jnp.where(self.words[i] > 0, self.lives[self.row(i)], 0)
         return (self.words[i] >> self.live_shift) & (2 * self.page_size - 1)
 
     def row(self, i):
@@ -252,7 +255,7 @@
 
 def remote_kernel(
     n_heads, sessions, recv_ref, key_hbm, value_hbm, out_ref,
-    meta, num, den, queries, words, key_buf, value_buf, sems,
+    meta, num, den, queries, lives, words, key_buf, value_buf, sems,
 ):
     devices, tiles, part_rows = recv_ref.shape[:3]
     rows = num.shape[1]
@@ -264,28 +267,33 @@
     head = lax.axis_index("heads")
     for d in range(n_dp):
         meta[0, d : d + 1, :] = decode(recv_ref, d * n_heads + head)
+    own = meta[0]
+    pages = Pages(
+        key_hbm, value_hbm, words, key_buf, value_buf, sems, num, den, places, lives
+    )
+    total = jnp.int32(0)
+    for d in range(n_dp):
+        for c in range(capacity):
+            slot = own[d, c]
+            for k in range(parts):
+                queries[total, k * part_rows : (k + 1) * part_rows] = recv_ref[
+                    d * n_heads + head, c * parts + k
+                ]
+            total = pages.add(total, slot > 0, pages.word(slot - 1, 0, d * places + c))
+
+    for d in range(n_dp):
         meta[1, d : d + 1, :] = longest_of(recv_ref, d, n_heads)
-    own, longest = meta[0], meta[1]
+    longest = meta[1]
     session = pltpu.roll(own, 128 - SESS_LANE, 1)
     page = pltpu.roll(own, 128 - PAGE_LANE, 1)
     length = jnp.zeros_like(own)
     for s in range(sessions):
         known = jnp.broadcast_to(longest[:, HIGH_LANE + s : HIGH_LANE + s + 1], own.shape)
         length = jnp.where(session == s, known, length)
-    live = jnp.clip(length - page * page_size, 0, page_size)
-    pages = Pages(key_hbm, value_hbm, words, key_buf, value_buf, sems, num, den, places)
-    device = lax.broadcasted_iota(jnp.int32, own.shape, 0)
-    place = lax.broadcasted_iota(jnp.int32, own.shape, 1) & (places - 1)
-    asked = jnp.where(own > 0, pages.word(own - 1, live, device * places + place), 0)
-    total = jnp.int32(0)
+    live = jnp.where(own > 0, jnp.clip(length - page * page_size, 0, page_size), 0)
     for d in range(n_dp):
         for c in range(capacity):
-            word = asked[d, c]
-            for k in range(parts):
-                queries[total, k * part_rows : (k + 1) * part_rows] = recv_ref[
-                    d * n_heads + head, c * parts + k
-                ]
-            total = pages.add(total, word > 0, word)
+            lives[d * places + c] = live[d, c]
     num[...] = jnp.zeros_like(num)
     den[...] = jnp.zeros_like(den)
     pages.run(total, lambda i: queries[i])
@@ -455,6 +463,7 @@
             pltpu.VMEM((n_dp * places, q_heads, head_dim), jnp.float32),
             pltpu.VMEM((n_dp, q_heads, head_dim), jnp.float32),
             pltpu.VMEM((asked + GROUP, q_heads, head_dim), jnp.bfloat16),
+            pltpu.SMEM((n_dp * places,), jnp.int32),
             *page_scratch(asked),
         ],
         compiler_params=page_limit(asked),

time: 34.8 us -> 34.5 us (level)
  Pallas kernels: 13.8 us -> 13 us
  waiting for transfers between devices: 1.43 us -> 1.8 us
    pallas_call x1, Pallas kernels: 6.61 us -> 6.21 us  [body(): pl.pallas_call(functools.partial(remote_kernel, n_heads, sessions), out_s...]
    all_to_all x1, waiting for transfers between devices: 1.43 us -> 1.8 us  [body(): lax.all_to_all(response, 'dp', split_axis=0, concat_axis=0, tiled=True)]
where the time goes in v4:
time: 34.5 us; the launch traced here: 34.1 us
  blocking collectives  15.9 us (46%)
  Pallas kernels  13 us (38%)
  starting transfers between devices  3.36 us (10%)
  waiting for transfers between devices  1.8 us (5%)
    all_to_all x1, blocking collectives, body(): lax.all_to_all(packed, ('dp', 'heads'), split_axis=0, concat_axis=0, tile...  15.9 us
    pallas_call x1, Pallas kernels, body(): pl.pallas_call(functools.partial(remote_kernel, n_heads, sessions), out_s...  6.21 us
    pallas_call x1, Pallas kernels, body(): pl.pallas_call(functools.partial(local_kernel, n_heads), out_shape=(accum...  4.95 us
    all_to_all x1, starting transfers between devices, body(): lax.all_to_all(response, 'dp', split_axis=0, concat_axis=0, tiled=True)  3.36 us
    all_to_all x1, waiting for transfers between devices, body(): lax.all_to_all(response, 'dp', split_axis=0, concat_axis=0, tiled=True)  1.8 us
    pallas_call x1, Pallas kernels, body(): pl.pallas_call(functools.partial(pack_kernel, n_heads), out_shape=jax.Sha...  1.11 us
    pallas_call x1, Pallas kernels, body(): pl.pallas_call(functools.partial(combine_kernel, capacity), out_shape=jax...  0.74 us
  transfers between devices with their start and end apart: 1, of which 1 were waited for; matrix products, arithmetic and copies ran while one was open for 0% of the time, Pallas kernels for 15%

profile of v4, /device:TPU:0, one launch (start us, length us, event | category | flops | bytes accessed | tf_op | source)
XLA Modules:
  0.0 34.1 jit_solution(1032409651135337849)
XLA Ops:
  0.0 1.1 %pack.1 = bf16[32,11,2,128]{3,2,1,0:T(2,128)(2,1)S(1)} custom-call(s32[1,8]{1,0:T(1,128)} %bitcast.6, s32[8,8]{1,0:T(8,128)} %table_hbm.3, s32[3,32]{1,0:T(4,128)} %bitcast.3, bf16[8,4,128]{2,1,0:T(4,128)(2,1)} %query_hbm.3), custom_call_target="tpu_custom_call" | custom-call | tf_op jit(solution)/shard_map/pack/pallas_call | solution.py:418
  1.1 15.9 %all_to_all.10.recv_ref = bf16[32,11,2,128]{3,2,1,0:T(2,128)(2,1)S(1)} all-to-all(bf16[32,11,2,128]{3,2,1,0:T(2,128)(2,1)S(1)} %pack.1), channel_id=1, replica_groups=mesh['dp'=8,'heads'=4] {'dp','heads'}, dimensions={0} | all-to-all | bytes 360448 | tf_op jit(solution)/shard_map/all_to_all | solution.py:438
  17.1 6.2 %remote_pages.1 = bf16[8,24,128]{2,1,0:T(8,128)(2,1)} custom-call(bf16[32,11,2,128]{3,2,1,0:T(2,128)(2,1)S(1)} %all_to_all.10.recv_ref, bf16[64,2,256,128]{3,2,1,0:T(8,128)(2,1)} %key_hbm.3, bf16[64,2,256,128]{3,2,1,0:T(8,128)(2,1)} %value_hbm.3), custom_call_target="tpu_custom_call" | custom-call | flops 100000000 | bytes 10000000 | tf_op jit(solution)/shard_map/remote_pages/pallas_call | solution.py:456
  23.3 3.4 %all-to-all-start.1 = ((bf16[8,24,128]{2,1,0:T(8,128)(2,1)}), bf16[8,24,128]{2,1,0:T(8,128)(2,1)S(1)}, u32[]{:S(2)}, u32[]{:S(2)}) async-start(bf16[8,24,128]{2,1,0:T(8,128)(2,1)} %remote_pages.1), calls=%async_computation.1 | async-start | bytes 98304 | tf_op jit(solution)/shard_map/all_to_all | solution.py:473
  26.6 4.9 %local_pages.1 = (f32[8,4,128]{2,1,0:T(4,128)S(1)}, f32[8,4,128]{2,1,0:T(4,128)S(1)}, bf16[32,192]{1,0:T(8,128)(2,1)S(1)}, s32[8,128]{1,0:T(8,128)S(1)}) custom-call(bf16[32,11,2,128]{3,2,1,0:T(2,128)(2,1)S(1)} %all_to_all.10.recv_ref, s32[8,8]{1,0:T(8,128)} %table_hbm.3, s32[3,32]{1,0:T(4,128)} %bitcast.4, s32[1,8]{1,0:T(1,128)} %bitcast.5, ...), custom_call_target="tpu_custom_call" | custom-call | flops 1000000000 | bytes 10000000 | tf_op jit(solution)/shard_map/local_pages/pallas_call | solution.py:476
  31.6 1.8 %all-to-all-done.1.back_ref = bf16[8,24,128]{2,1,0:T(8,128)(2,1)S(1)} async-done(((bf16[8,24,128]{2,1,0:T(8,128)(2,1)}), bf16[8,24,128]{2,1,0:T(8,128)(2,1)S(1)}, u32[]{:S(2)}, u32[]{:S(2)}) %all-to-all-start.1) | async-done | bytes 49184 | tf_op jit(solution)/shard_map/all_to_all | solution.py:473
  33.4 0.7 %combine.1 = bf16[8,4,128]{2,1,0:T(4,128)(2,1)} custom-call(bf16[8,24,128]{2,1,0:T(8,128)(2,1)S(1)} %all-to-all-done.1.back_ref, f32[8,4,128]{2,1,0:T(4,128)S(1)} %get-tuple-element.9.num_ref, f32[8,4,128]{2,1,0:T(4,128)S(1)} %get-tuple-element.10.den_ref, bf16[32,192]{1,0:T(8,128)(2,1)S(1)} %get-tuple-element.11.spread_ref, ...), custom_call_target="tpu_custom_call" | custom-call | tf_op jit(solution)/shard_map/combine/pallas_call | solution.py:501
Async XLA Ops:
  23.3 10.1 %all-to-all-start.1 = ((bf16[8,24,128]{2,1,0:T(8,128)(2,1)}), bf16[8,24,128]{2,1,0:T(8,128)(2,1)S(1)}, u32[]{:S(2)}, u32[]{:S(2)}) async-start(bf16[8,24,128]{2,1,0:T(8,128)(2,1)} %remote_pages.1), calls=%async_computation.1 | async-start | bytes 98304 | tf_op jit(solution)/shard_map/all_to_all | solution.py:473

commit v5 on v4

--- a/solution.py
+++ b/solution.py
@@ -12,7 +12,8 @@
 score_divisor = 12.0
 exp_scale = softcap_limit * math.log2(math.e)
 GROUP = 5
-LEN_BASE = 128
+LEN_BITS = 7
+LEN_BASE = 1 << LEN_BITS
 SMALL_VMEM = 4 << 20
 SESS_LANE, PAGE_LANE, HIGH_LANE, LOW_LANE = 32, 64, 96, 112
 
@@ -50,16 +51,18 @@
     base = jnp.zeros((1, 128), jnp.int32)
     for d in range(n_dp):
         count[d] = 0
-    for copy in copies:
+    for copy in copies[:2]:
         copy.wait()
     for s in range(sessions):
         length = len_ref[0, s]
-        base = jnp.where(lane == HIGH_LANE + s, length // LEN_BASE, base)
-        base = jnp.where(lane == LOW_LANE + s, length % LEN_BASE, base)
+        base = jnp.where(lane == HIGH_LANE + s, length >> LEN_BITS, base)
+        base = jnp.where(lane == LOW_LANE + s, length & (LEN_BASE - 1), base)
         for p in range(pages_max):
             owner[table_ref[s, p]] = s * 256 + p
     for d in range(n_dp):
         meta[d] = base
+    for copy in copies[2:]:
+        copy.wait()
     for r in range(moves):
         source = plan_ref[0, r]
         rank = count[source]

time: 34.5 us -> 34.2 us (level)
  transfers between devices with their start and end apart: 1 -> 1, of which waited for: 1 -> 1; matrix products, arithmetic and copies ran while one was open for 0% -> 0% of each run, Pallas kernels for 15% -> 16%
where the time goes in v5:
time: 34.2 us; the launch traced here: 33.8 us
  blocking collectives  15.9 us (46%)
  Pallas kernels  13 us (38%)
  starting transfers between devices  3.36 us (10%)
  waiting for transfers between devices  1.48 us (4%)
    all_to_all x1, blocking collectives, body(): lax.all_to_all(packed, ('dp', 'heads'), split_axis=0, concat_axis=0, tile...  15.9 us
    pallas_call x1, Pallas kernels, body(): pl.pallas_call(functools.partial(remote_kernel, n_heads, sessions), out_s...  5.97 us
    pallas_call x1, Pallas kernels, body(): pl.pallas_call(functools.partial(local_kernel, n_heads), out_shape=(accum...  5.25 us
    all_to_all x1, starting transfers between devices, body(): lax.all_to_all(response, 'dp', split_axis=0, concat_axis=0, tiled=True)  3.36 us
    all_to_all x1, waiting for transfers between devices, body(): lax.all_to_all(response, 'dp', split_axis=0, concat_axis=0, tiled=True)  1.48 us
    pallas_call x1, Pallas kernels, body(): pl.pallas_call(functools.partial(pack_kernel, n_heads), out_shape=jax.Sha...  1.05 us
    pallas_call x1, Pallas kernels, body(): pl.pallas_call(functools.partial(combine_kernel, capacity), out_shape=jax...  0.74 us
  transfers between devices with their start and end apart: 1, of which 1 were waited for; matrix products, arithmetic and copies ran while one was open for 0% of the time, Pallas kernels for 16%

profile of v5, /device:TPU:0, one launch (start us, length us, event | category | flops | bytes accessed | tf_op | source)
XLA Modules:
  0.0 33.8 jit_solution(1634274394428560211)
XLA Ops:
  0.0 1.1 %pack.1 = bf16[32,11,2,128]{3,2,1,0:T(2,128)(2,1)S(1)} custom-call(s32[1,8]{1,0:T(1,128)} %bitcast.6, s32[8,8]{1,0:T(8,128)} %table_hbm.3, s32[3,32]{1,0:T(4,128)} %bitcast.3, bf16[8,4,128]{2,1,0:T(4,128)(2,1)} %query_hbm.3), custom_call_target="tpu_custom_call" | custom-call | tf_op jit(solution)/shard_map/pack/pallas_call | solution.py:421
  1.1 15.9 %all_to_all.10.recv_ref = bf16[32,11,2,128]{3,2,1,0:T(2,128)(2,1)S(1)} all-to-all(bf16[32,11,2,128]{3,2,1,0:T(2,128)(2,1)S(1)} %pack.1), channel_id=1, replica_groups=mesh['dp'=8,'heads'=4] {'dp','heads'}, dimensions={0} | all-to-all | bytes 360448 | tf_op jit(solution)/shard_map/all_to_all | solution.py:441
  17.0 6.0 %remote_pages.1 = bf16[8,24,128]{2,1,0:T(8,128)(2,1)} custom-call(bf16[32,11,2,128]{3,2,1,0:T(2,128)(2,1)S(1)} %all_to_all.10.recv_ref, bf16[64,2,256,128]{3,2,1,0:T(8,128)(2,1)} %key_hbm.3, bf16[64,2,256,128]{3,2,1,0:T(8,128)(2,1)} %value_hbm.3), custom_call_target="tpu_custom_call" | custom-call | flops 100000000 | bytes 10000000 | tf_op jit(solution)/shard_map/remote_pages/pallas_call | solution.py:459
  23.0 3.4 %all-to-all-start.1 = ((bf16[8,24,128]{2,1,0:T(8,128)(2,1)}), bf16[8,24,128]{2,1,0:T(8,128)(2,1)S(1)}, u32[]{:S(2)}, u32[]{:S(2)}) async-start(bf16[8,24,128]{2,1,0:T(8,128)(2,1)} %remote_pages.1), calls=%async_computation.1 | async-start | bytes 98304 | tf_op jit(solution)/shard_map/all_to_all | solution.py:476
  26.3 5.2 %local_pages.1 = (f32[8,4,128]{2,1,0:T(4,128)S(1)}, f32[8,4,128]{2,1,0:T(4,128)S(1)}, bf16[32,192]{1,0:T(8,128)(2,1)S(1)}, s32[8,128]{1,0:T(8,128)S(1)}) custom-call(bf16[32,11,2,128]{3,2,1,0:T(2,128)(2,1)S(1)} %all_to_all.10.recv_ref, s32[8,8]{1,0:T(8,128)} %table_hbm.3, s32[3,32]{1,0:T(4,128)} %bitcast.4, s32[1,8]{1,0:T(1,128)} %bitcast.5, ...), custom_call_target="tpu_custom_call" | custom-call | flops 1000000000 | bytes 10000000 | tf_op jit(solution)/shard_map/local_pages/pallas_call | solution.py:479
  31.6 1.5 %all-to-all-done.1.back_ref = bf16[8,24,128]{2,1,0:T(8,128)(2,1)S(1)} async-done(((bf16[8,24,128]{2,1,0:T(8,128)(2,1)}), bf16[8,24,128]{2,1,0:T(8,128)(2,1)S(1)}, u32[]{:S(2)}, u32[]{:S(2)}) %all-to-all-start.1) | async-done | bytes 49184 | tf_op jit(solution)/shard_map/all_to_all | solution.py:476
  33.1 0.7 %combine.1 = bf16[8,4,128]{2,1,0:T(4,128)(2,1)} custom-call(bf16[8,24,128]{2,1,0:T(8,128)(2,1)S(1)} %all-to-all-done.1.back_ref, f32[8,4,128]{2,1,0:T(4,128)S(1)} %get-tuple-element.9.num_ref, f32[8,4,128]{2,1,0:T(4,128)S(1)} %get-tuple-element.10.den_ref, bf16[32,192]{1,0:T(8,128)(2,1)S(1)} %get-tuple-element.11.spread_ref, ...), custom_call_target="tpu_custom_call" | custom-call | tf_op jit(solution)/shard_map/combine/pallas_call | solution.py:504
Async XLA Ops:
  23.0 10.1 %all-to-all-start.1 = ((bf16[8,24,128]{2,1,0:T(8,128)(2,1)}), bf16[8,24,128]{2,1,0:T(8,128)(2,1)S(1)}, u32[]{:S(2)}, u32[]{:S(2)}) async-start(bf16[8,24,128]{2,1,0:T(8,128)(2,1)} %remote_pages.1), calls=%async_computation.1 | async-start | bytes 98304 | tf_op jit(solution)/shard_map/all_to_all | solution.py:476

commit v6 on v5

--- a/solution.py
+++ b/solution.py
@@ -11,7 +11,7 @@
 softcap_limit = 50.0
 score_divisor = 12.0
 exp_scale = softcap_limit * math.log2(math.e)
-GROUP = 5
+GROUP = 7
 LEN_BITS = 7
 LEN_BASE = 1 << LEN_BITS
 SMALL_VMEM = 4 << 20

time: 34.2 us -> 34.4 us (level)
  Pallas kernels: 13 us -> 14 us
  waiting for transfers between devices: 1.48 us -> 0.79 us
    pallas_call x1, Pallas kernels: 5.25 us -> 5.93 us  [body(): pl.pallas_call(functools.partial(local_kernel, n_heads), out_shape=(accum...]
    all_to_all x1, waiting for transfers between devices: 1.48 us -> 0.79 us  [body(): lax.all_to_all(response, 'dp', split_axis=0, concat_axis=0, tiled=True)]
  transfers between devices with their start and end apart: 1 -> 1, of which waited for: 1 -> 1; matrix products, arithmetic and copies ran while one was open for 0% -> 0% of each run, Pallas kernels for 16% -> 17%
where the time goes in v6:
time: 34.4 us; the launch traced here: 34.1 us
  blocking collectives  15.9 us (46%)
  Pallas kernels  14 us (41%)
  starting transfers between devices  3.36 us (10%)
  waiting for transfers between devices  0.79 us (2%)
    all_to_all x1, blocking collectives, body(): lax.all_to_all(packed, ('dp', 'heads'), split_axis=0, concat_axis=0, tile...  15.9 us
    pallas_call x1, Pallas kernels, body(): pl.pallas_call(functools.partial(remote_kernel, n_heads, sessions), out_s...  6.26 us
    pallas_call x1, Pallas kernels, body(): pl.pallas_call(functools.partial(local_kernel, n_heads), out_shape=(accum...  5.93 us
    all_to_all x1, starting transfers between devices, body(): lax.all_to_all(response, 'dp', split_axis=0, concat_axis=0, tiled=True)  3.36 us
    pallas_call x1, Pallas kernels, body(): pl.pallas_call(functools.partial(pack_kernel, n_heads), out_shape=jax.Sha...  1.05 us
    all_to_all x1, waiting for transfers between devices, body(): lax.all_to_all(response, 'dp', split_axis=0, concat_axis=0, tiled=True)  0.79 us
    pallas_call x1, Pallas kernels, body(): pl.pallas_call(functools.partial(combine_kernel, capacity), out_shape=jax...  0.74 us
  transfers between devices with their start and end apart: 1, of which 1 were waited for; matrix products, arithmetic and copies ran while one was open for 0% of the time, Pallas kernels for 17%

profile of v6, /device:TPU:0, one launch (start us, length us, event | category | flops | bytes accessed | tf_op | source)
XLA Modules:
  0.0 34.1 jit_solution(12346004375435772712)
XLA Ops:
  0.0 1.1 %pack.1 = bf16[32,11,2,128]{3,2,1,0:T(2,128)(2,1)S(1)} custom-call(s32[1,8]{1,0:T(1,128)} %bitcast.6, s32[8,8]{1,0:T(8,128)} %table_hbm.3, s32[3,32]{1,0:T(4,128)} %bitcast.3, bf16[8,4,128]{2,1,0:T(4,128)(2,1)} %query_hbm.3), custom_call_target="tpu_custom_call" | custom-call | tf_op jit(solution)/shard_map/pack/pallas_call | solution.py:421
  1.1 15.9 %all_to_all.10.recv_ref = bf16[32,11,2,128]{3,2,1,0:T(2,128)(2,1)S(1)} all-to-all(bf16[32,11,2,128]{3,2,1,0:T(2,128)(2,1)S(1)} %pack.1), channel_id=1, replica_groups=mesh['dp'=8,'heads'=4] {'dp','heads'}, dimensions={0} | all-to-all | bytes 360448 | tf_op jit(solution)/shard_map/all_to_all | solution.py:441
  17.0 6.3 %remote_pages.1 = bf16[8,24,128]{2,1,0:T(8,128)(2,1)} custom-call(bf16[32,11,2,128]{3,2,1,0:T(2,128)(2,1)S(1)} %all_to_all.10.recv_ref, bf16[64,2,256,128]{3,2,1,0:T(8,128)(2,1)} %key_hbm.3, bf16[64,2,256,128]{3,2,1,0:T(8,128)(2,1)} %value_hbm.3), custom_call_target="tpu_custom_call" | custom-call | flops 100000000 | bytes 10000000 | tf_op jit(solution)/shard_map/remote_pages/pallas_call | solution.py:459
  23.3 3.4 %all-to-all-start.1 = ((bf16[8,24,128]{2,1,0:T(8,128)(2,1)}), bf16[8,24,128]{2,1,0:T(8,128)(2,1)S(1)}, u32[]{:S(2)}, u32[]{:S(2)}) async-start(bf16[8,24,128]{2,1,0:T(8,128)(2,1)} %remote_pages.1), calls=%async_computation.1 | async-start | bytes 98304 | tf_op jit(solution)/shard_map/all_to_all | solution.py:476
  26.6 5.9 %local_pages.1 = (f32[8,4,128]{2,1,0:T(4,128)S(1)}, f32[8,4,128]{2,1,0:T(4,128)S(1)}, bf16[32,192]{1,0:T(8,128)(2,1)S(1)}, s32[8,128]{1,0:T(8,128)S(1)}) custom-call(bf16[32,11,2,128]{3,2,1,0:T(2,128)(2,1)S(1)} %all_to_all.10.recv_ref, s32[8,8]{1,0:T(8,128)} %table_hbm.3, s32[3,32]{1,0:T(4,128)} %bitcast.4, s32[1,8]{1,0:T(1,128)} %bitcast.5, ...), custom_call_target="tpu_custom_call" | custom-call | flops 1000000000 | bytes 10000000 | tf_op jit(solution)/shard_map/local_pages/pallas_call | solution.py:479
  32.6 0.8 %all-to-all-done.1.back_ref = bf16[8,24,128]{2,1,0:T(8,128)(2,1)S(1)} async-done(((bf16[8,24,128]{2,1,0:T(8,128)(2,1)}), bf16[8,24,128]{2,1,0:T(8,128)(2,1)S(1)}, u32[]{:S(2)}, u32[]{:S(2)}) %all-to-all-start.1) | async-done | bytes 49184 | tf_op jit(solution)/shard_map/all_to_all | solution.py:476
  33.4 0.7 %combine.1 = bf16[8,4,128]{2,1,0:T(4,128)(2,1)} custom-call(bf16[8,24,128]{2,1,0:T(8,128)(2,1)S(1)} %all-to-all-done.1.back_ref, f32[8,4,128]{2,1,0:T(4,128)S(1)} %get-tuple-element.9.num_ref, f32[8,4,128]{2,1,0:T(4,128)S(1)} %get-tuple-element.10.den_ref, bf16[32,192]{1,0:T(8,128)(2,1)S(1)} %get-tuple-element.11.spread_ref, ...), custom_call_target="tpu_custom_call" | custom-call | tf_op jit(solution)/shard_map/combine/pallas_call | solution.py:504
Async XLA Ops:
  23.3 10.1 %all-to-all-start.1 = ((bf16[8,24,128]{2,1,0:T(8,128)(2,1)}), bf16[8,24,128]{2,1,0:T(8,128)(2,1)S(1)}, u32[]{:S(2)}, u32[]{:S(2)}) async-start(bf16[8,24,128]{2,1,0:T(8,128)(2,1)} %remote_pages.1), calls=%async_computation.1 | async-start | bytes 98304 | tf_op jit(solution)/shard_map/all_to_all | solution.py:476
